TPU v7x, 256 devices: a whole 4x4x8 slice. The times are simulated.
256 devices in a mesh: zero: 32 (over z, y), tp: 8 (over x, core).
Axes of the slice: x: 4, y: 4, z: 8, core: 2. Of those that a mesh axis runs over, the one named last changes fastest.
Arguments:
- train_gate: bfloat16 [3072, 8192], P('zero', 'tp'), may hold values from -0.109375 to 0.109375
- low_gate: bfloat16 [3072, 16], P('zero'), may hold values from -0.109375 to 0.109375
- high_gate: bfloat16 [16, 8192], P(None, 'tp'), may hold values from -1.5 to 1.5
- train_up: bfloat16 [3072, 8192], P('zero', 'tp'), may hold values from -0.109375 to 0.109375
- low_up: bfloat16 [3072, 16], P('zero'), may hold values from -0.109375 to 0.109375
- high_up: bfloat16 [16, 8192], P(None, 'tp'), may hold values from -1.5 to 1.5
- train_down: bfloat16 [8192, 3072], P('tp', 'zero'), may hold values from -0.0625 to 0.0625
- low_down: bfloat16 [8192, 16], P('tp'), may hold values from -0.0625 to 0.0625
- high_down: bfloat16 [16, 3072], P(None, 'zero'), may hold values from -1.5 to 1.5
- norm_train: float32 [3072], P(('zero', 'tp')), may hold values from 0.25 to 1.75
- norm_step: float32 [3072], P(('zero', 'tp')), may hold values from -0.3 to 0.3
Outputs:
- serve_gate: bfloat16 [8192, 3072], P('tp')
- serve_up: bfloat16 [8192, 3072], P('tp')
- serve_down: bfloat16 [3072, 8192], P(None, 'tp')
- serve_norm: bfloat16 [3072], replicated
All inputs are finite; a program needn't handle non-finite values.
Results may differ from a plain program's by a relative error of at most 0.001.
Values may be sent and summed in bfloat16 or wider, within the bound.
No kernel may reach another device: no remote copies, remote signals or barrier semaphores. Data moves between devices by JAX's collectives and lax.ppermute only.
A program may use at most 128 MiB of HBM per device.

v0:
```python
import functools

import jax
import jax.numpy as jnp
from jax import lax
from jax.experimental import pallas as pl
from jax.experimental.pallas import tpu as pltpu
from jax.sharding import Mesh
from jax.sharding import PartitionSpec as P


ZERO = ("zero_0", "zero_1")
ZERO_TP = ("zero_0", "zero_1", "tp_0", "tp_1")
TP = ("tp_0", "tp_1")
NZ, NY = 8, 4
D_MODEL, D_INNER, RANK = 3072, 8192, 16


mix_rate = 0.5

ROWS = 96
BLOCK = NY * ROWS
WIDE = 1024
CUT = 128
A_COLS = WIDE + CUT
B_COLS = WIDE + WIDE - CUT
STEP = 128

ANY = pl.BlockSpec(memory_space=pl.ANY)
VMEM = pl.BlockSpec(memory_space=pltpu.VMEM)


def shifted(x, axis, step):
    n = {"zero_0": NZ, "zero_1": NY, "tp_0": 4, "tp_1": 2}[axis]
    return lax.ppermute(x, axis, [(i, (i + step) % n) for i in range(n)])


def merged(train, low, high):
    product = lax.dot_general(
        low, high, (((0,), (0,)), ((), ())), preferred_element_type=jnp.float32
    )
    return (train.astype(jnp.float32) + mix_rate * product).astype(jnp.bfloat16)


def merge_body(tg, lg, hg, td, ld, hd, tu, lu, hu, out_a, out_b):
    up = merged(tu[...], lu[...], hu[...])
    out_a[:, :WIDE] = merged(tg[...], lg[...], hg[...])
    out_a[:, WIDE:] = up[:, :CUT]
    out_b[:, :WIDE] = merged(td[...], ld[...], hd[...])
    out_b[:, WIDE:] = up[:, CUT:]


def merge_call(*args):
    return pl.pallas_call(
        merge_body,
        out_shape=(
            jax.ShapeDtypeStruct((ROWS, A_COLS), jnp.bfloat16),
            jax.ShapeDtypeStruct((ROWS, B_COLS), jnp.bfloat16),
        ),
        in_specs=[VMEM] * len(args),
        out_specs=(VMEM, VMEM),
    )(*args)


def stack_body(starts, *refs):
    pieces, out, sems = refs[:-2], refs[-2], refs[-1]
    y = lax.axis_index("zero_1")
    copies = []
    for k, piece in enumerate(pieces):
        rel, row = starts[k]
        at = row if rel is None else lax.rem(y + rel, NY) * ROWS + row
        at = at if rel is None else pl.multiple_of(at, 16)
        copies.append(
            pltpu.make_async_copy(
                piece, out.at[pl.ds(at, piece.shape[0])], sems.at[k]
            )
        )
    for c in copies:
        c.start()
    for c in copies:
        c.wait()


def stacked(pieces, starts):
    rows = sum(p.shape[0] for p in pieces)
    nbytes = rows * pieces[0].shape[1] * 4
    return pl.pallas_call(
        functools.partial(stack_body, starts),
        out_shape=jax.ShapeDtypeStruct((rows, pieces[0].shape[1]), jnp.bfloat16),
        in_specs=[ANY] * len(pieces),
        out_specs=VMEM,
        scratch_shapes=[pltpu.SemaphoreType.DMA((len(pieces),))],
        cost_estimate=pl.CostEstimate(
            flops=nbytes * 100, bytes_accessed=nbytes, transcendentals=0
        ),
    )(*pieces)


def place_body(first, kind, blocks, nsrc, *refs):
    srcs = refs[:nsrc]
    outs = refs[nsrc + (0 if first else 3) :][:3]
    held, turned, in_sem, out_sem = refs[-4:]
    gate, up, down = outs
    z, y = lax.axis_index("zero_0"), lax.axis_index("zero_1")
    taken, loads = 0, []
    for b, (_, parts) in enumerate(blocks):
        mine = []
        for src, srow, rows, rel, row in parts:
            at = row
            if rel is not None:
                at = pl.multiple_of(lax.rem(y + rel, NY) * ROWS + row, 16)
            c = pltpu.make_async_copy(
                srcs[src].at[pl.ds(srow, rows)],
                held.at[b, pl.ds(at, rows)],
                in_sem.at[taken],
            )
            c.start()
            mine.append(c)
            taken += 1
        loads.append(mine)
    stores = []
    for b, (zrel, _) in enumerate(blocks):
        for c in loads[b]:
            c.wait()
        zabs = lax.rem(z + zrel, NZ)
        cols = pl.ds(pl.multiple_of(zabs * BLOCK, 128), BLOCK)
        if kind == "b":
            c = pltpu.make_async_copy(
                held.at[b, :, pl.ds(0, WIDE)], down.at[cols], out_sem.at[b, 0]
            )
            c.start()
            stores.append(c)
            groups = [(WIDE, WIDE - CUT, up, CUT, 1)]
        else:
            groups = [(0, WIDE, gate, 0, 0), (WIDE, CUT, up, 0, 1)]
        for start, width, out, row, k in groups:
            base = start if kind == "a" else start - WIDE

            def turn(i, _, start=start, base=base, b=b):
                src = pl.multiple_of(start + i * STEP, STEP)
                dst = pl.multiple_of(base + i * STEP, STEP)
                turned[b, pl.ds(dst, STEP), :] = held[b, :, pl.ds(src, STEP)].T
                return 0

            lax.fori_loop(0, width // STEP, turn, 0)
            c = pltpu.make_async_copy(
                turned.at[b, pl.ds(base, width)],
                out.at[pl.ds(row, width), cols],
                out_sem.at[b, k],
            )
            c.start()
            stores.append(c)
    for c in stores:
        c.wait()


OUT_SHAPES = (
    jax.ShapeDtypeStruct((WIDE, NZ * BLOCK), jnp.bfloat16),
    jax.ShapeDtypeStruct((WIDE, NZ * BLOCK), jnp.bfloat16),
    jax.ShapeDtypeStruct((NZ * BLOCK, WIDE), jnp.bfloat16),
)


def placed(outs, kind, blocks, srcs):
    first = outs is None
    n = len(blocks)
    cols = A_COLS if kind == "a" else B_COLS
    tall = A_COLS if kind == "a" else WIDE - CUT
    extra = () if first else tuple(outs)
    nbytes = n * BLOCK * cols * 4
    return pl.pallas_call(
        functools.partial(place_body, first, kind, blocks, len(srcs)),
        out_shape=OUT_SHAPES,
        in_specs=[ANY] * (len(srcs) + len(extra)),
        out_specs=[ANY] * 3,
        input_output_aliases={}
        if first
        else {len(srcs) + k: k for k in range(3)},
        scratch_shapes=[
            pltpu.VMEM((n, BLOCK, cols), jnp.bfloat16),
            pltpu.VMEM((n, tall, BLOCK), jnp.bfloat16),
            pltpu.SemaphoreType.DMA((sum(len(b[1]) for b in blocks),)),
            pltpu.SemaphoreType.DMA((n, 2)),
        ],
        cost_estimate=pl.CostEstimate(
            flops=nbytes * 200, bytes_accessed=nbytes, transcendentals=0
        ),
    )(*srcs, *extra)


def per_device(
    train_gate,
    low_gate,
    high_gate,
    train_up,
    low_up,
    high_up,
    train_down,
    low_down,
    high_down,
    norm_train,
    norm_step,
):
    z, y = "zero_0", "zero_1"
    half, mid, part = ROWS // 2, BLOCK // 2, 3 * ROWS // 2

    gain = (norm_train + norm_step).astype(jnp.bfloat16)
    place = lax.axis_index(ZERO_TP) * gain.shape[0]
    full = lax.dynamic_update_slice(
        jnp.zeros((gain.shape[0] * 256,), jnp.bfloat16), gain, (place,)
    )

    def doubled(full, axis, step):
        return full + shifted(full, axis, step)

    def b_blocks(rels):
        return tuple(
            (
                rel,
                tuple(
                    (s, i * ROWS, ROWS, yrel, 0) for s, yrel in enumerate((0, 3, 1, 2))
                ),
            )
            for i, rel in enumerate(rels)
        )

    def a_block(rel, s):
        return (rel, ((s, 0, BLOCK, None, 0),))

    own_a, own_b = merge_call(
        train_gate,
        low_gate.T,
        high_gate,
        train_down.T,
        high_down,
        low_down.T,
        train_up,
        low_up.T,
        high_up,
    )
    a_l = shifted(own_a, y, 1)
    a_r = shifted(own_a, y, -1)
    f1 = shifted(own_b, z, 1)
    g1 = shifted(own_b, z, -1)
    l0 = shifted(own_b, y, 1)
    full = doubled(full, "tp_1", 1)
    a_f = shifted(a_r, y, -1)
    r0 = shifted(own_b, y, -1)
    f2 = shifted(f1, z, 1)
    g2 = shifted(g1, z, -1)
    s1 = stacked((f1, g1), ((None, 0), (None, 96)))
    l1 = shifted(s1, y, 1)
    r1 = shifted(s1, y, -1)
    block = stacked((own_a, a_l, a_r, a_f), ((0, 0), (3, 0), (1, 0), (2, 0)))
    p1 = shifted(block, z, 1)
    q1 = shifted(block, z, -1)
    o0 = shifted(l0, y, 1)
    full = doubled(full, "tp_0", 1)
    f3 = shifted(f2, z, 1)
    g3 = shifted(g2, z, -1)
    s2 = stacked((f2, g2), ((None, 0), (None, 96)))
    l2 = shifted(s2, y, 1)
    r2 = shifted(s2, y, -1)
    full = doubled(full, "tp_0", 2)
    outs = placed(None, "a", (a_block(0, 0),), (block,))
    o1 = shifted(r1, y, -1)
    full = doubled(full, y, 1)
    outs = placed(outs, "b", b_blocks((0,)), (own_b, l0, r0, o0))
    f4 = shifted(f3[:half], z, 1)
    g4 = shifted(g3[half:], z, -1)
    p2 = shifted(p1, z, 1)
    q2 = shifted(q1, z, -1)
    full = doubled(full, y, 2)
    outs = placed(outs, "a", (a_block(7, 0), a_block(1, 1)), (p1, q1))
    o2 = shifted(l2, y, 1)
    s3 = stacked((f3, g3, f4, g4), ((None, 0), (None, 96), (None, 192), (None, 240)))
    l3 = shifted(s3, y, 1)
    r3 = shifted(s3, y, -1)
    full = doubled(full, z, 1)
    outs = placed(outs, "b", b_blocks((7, 1)), (s1, l1, r1, o1))
    p3 = shifted(p2, z, 1)
    q3 = shifted(q2, z, -1)
    full = doubled(full, z, 2)
    outs = placed(outs, "a", (a_block(6, 0), a_block(2, 1)), (p2, q2))
    outs = placed(outs, "b", b_blocks((6, 2)), (s2, l2, r2, o2))
    full = doubled(full, z, 4)
    t3 = shifted(l3[:part], y, 1)
    b3 = shifted(r3[part:], y, -1)
    p4 = shifted(p3[:mid], z, 1)
    q4 = shifted(q3[mid:], z, -1)
    outs = placed(outs, "a", (a_block(5, 0), a_block(3, 1)), (p3, q3))
    near = [[(s, i * ROWS, ROWS, r, 0) for s, r in enumerate((0, 3, 1))] for i in range(3)]
    far = (
        [(3, 0, ROWS, 2, 0)],
        [(3, ROWS, half, 2, 0), (4, 0, half, 2, half)],
        [(4, half, ROWS, 2, 0)],
    )
    outs = placed(
        outs,
        "b",
        tuple(
            (rel, tuple(n + f)) for rel, n, f in zip((5, 3, 4), near, far, strict=True)
        ),
        (s3, l3, r3, t3, b3),
    )
    outs = placed(
        outs, "a", ((4, ((0, 0, mid, None, 0), (1, 0, mid, None, mid))),), (p4, q4)
    )
    return (*outs, full)


def solution(mesh):
    finer = Mesh(mesh.devices.reshape(8, 4, 4, 2), ("zero_0", "zero_1", "tp_0", "tp_1"))
    in_specs = (
        P(ZERO, TP),
        P(ZERO, None),
        P(None, TP),
        P(ZERO, TP),
        P(ZERO, None),
        P(None, TP),
        P(TP, ZERO),
        P(TP, None),
        P(None, ZERO),
        P(ZERO_TP),
        P(ZERO_TP),
    )
    out_specs = (P(TP, None), P(TP, None), P(None, TP), P())

    step = jax.shard_map(
        per_device, mesh=finer, in_specs=in_specs, out_specs=out_specs, check_vma=False
    )
    low, wide = D_MODEL, D_INNER
    shapes = ((low, wide), (low, RANK), (RANK, wide)) * 2
    shapes += ((wide, low), (wide, RANK), (RANK, low))
    jax.eval_shape(
        step,
        *(jax.ShapeDtypeStruct(s, jnp.bfloat16) for s in shapes),
        *(jax.ShapeDtypeStruct((low,), jnp.float32) for _ in range(2)),
    )
    return step
```

profile of v0, /device:TPU:8, one launch (start us, length us, event | category | flops | bytes accessed | tf_op | source)
XLA Modules:
  0.0 208.4 jit_solution(11962090423567881689)
XLA Ops:
  0.6 2.3 %shard_map.138 = (bf16[96,1152]{1,0:T(8,128)(2,1)}, bf16[96,1920]{1,0:T(8,128)(2,1)}) custom-call(bf16[96,1024]{1,0:T(8,128)(2,1)} %tg.1, bf16[16,96]{1,0:T(8,128)(2,1)} %bitcast.6, bf16[16,1024]{1,0:T(8,128)(2,1)} %hg.1, bf16[96,1024]{1,0:T(8,128)(2,1)} %bitcast.4, bf16[16,96]{1,0:T(8,128)(2,1)} %ld.1, bf16[16,1024]{1,0:T(8,128)(2,1)} %bitcast.5, ...), custom_call_target="tpu_custom_call" | custom-call | tf_op jit(solution)/shard_map/pallas_call | solution.py:54
  4.9 3.9 %collective-permute-start.14 = (bf16[96,1920]{1,0:T(8,128)(2,1)}, bf16[96,1920]{1,0:T(8,128)(2,1)S(1)}, u32[]{:S(2)}, u32[]{:S(2)}) collective-permute-start(bf16[96,1920]{1,0:T(8,128)(2,1)} %get-tuple-element.34.refs_0_), channel_id=1, source_target_pairs={{0,224},{32,0},{64,32},{96,64},{128,96},{160,128},{192,160},{224,1... | collective-permute-start | bytes 1105928 | tf_op jit(solution)/shard_map/ppermute | solution.py:35
  11.9 5.7 %collective-permute-done.11.refs_0_ = bf16[96,1920]{1,0:T(8,128)(2,1)S(1)} collective-permute-done((bf16[96,1920]{1,0:T(8,128)(2,1)}, bf16[96,1920]{1,0:T(8,128)(2,1)S(1)}, u32[]{:S(2)}, u32[]{:S(2)}) %collective-permute-start.11) | collective-permute-done | bytes 368672 | tf_op jit(solution)/shard_map/ppermute | solution.py:35
  17.6 3.2 %collective-permute-start.15 = (bf16[96,1920]{1,0:T(8,128)(2,1)S(1)}, bf16[96,1920]{1,0:T(8,128)(2,1)}, u32[]{:S(2)}, u32[]{:S(2)}) collective-permute-start(bf16[96,1920]{1,0:T(8,128)(2,1)S(1)} %collective-permute-done.14.refs_1_), channel_id=1, source_target_pairs={{0,224},{32,0},{64,32},{96,64},{128,96},{160,128},{192,160},{224,1... | collective-permute-start | bytes 1105928 | tf_op jit(solution)/shard_map/ppermute | solution.py:35
  22.6 3.4 %collective-permute-done.33 = bf16[3072]{0:T(1024)(128)(2,1)S(1)} collective-permute-done((bf16[3072]{0:T(1024)(128)(2,1)S(1)}, bf16[3072]{0:T(1024)(128)(2,1)S(1)}, u32[]{:S(2)}, u32[]{:S(2)}) %collective-permute-start.33) | collective-permute-done | bytes 6176 | tf_op jit(solution)/shard_map/ppermute | solution.py:35
  27.8 3.3 %collective-permute-done.34 = bf16[3072]{0:T(1024)(128)(2,1)S(1)} collective-permute-done((bf16[3072]{0:T(1024)(128)(2,1)S(1)}, bf16[3072]{0:T(1024)(128)(2,1)S(1)}, u32[]{:S(2)}, u32[]{:S(2)}) %collective-permute-start.34) | collective-permute-done | bytes 6176 | tf_op jit(solution)/shard_map/ppermute | solution.py:35
  34.8 2.3 %collective-permute-start.36 = (bf16[3072]{0:T(1024)(128)(2,1)S(1)}, bf16[3072]{0:T(1024)(128)(2,1)S(1)}, u32[]{:S(2)}, u32[]{:S(2)}) collective-permute-start(bf16[3072]{0:T(1024)(128)(2,1)S(1)} %add.48), channel_id=1, source_target_pairs={{0,16},{8,24},{16,0},{24,8},{1,17},{9,25},{17,1},{25,9},{2,18},{10... | collective-permute-start | bytes 18440 | tf_op jit(solution)/shard_map/ppermute | solution.py:35
  37.1 2.8 %collective-permute-done.36 = bf16[3072]{0:T(1024)(128)(2,1)S(1)} collective-permute-done((bf16[3072]{0:T(1024)(128)(2,1)S(1)}, bf16[3072]{0:T(1024)(128)(2,1)S(1)}, u32[]{:S(2)}, u32[]{:S(2)}) %collective-permute-start.36) | collective-permute-done | bytes 6176 | tf_op jit(solution)/shard_map/ppermute | solution.py:35
  39.9 4.8 %collective-permute-done.37 = bf16[3072]{0:T(1024)(128)(2,1)S(1)} collective-permute-done((bf16[3072]{0:T(1024)(128)(2,1)S(1)}, bf16[3072]{0:T(1024)(128)(2,1)S(1)}, u32[]{:S(2)}, u32[]{:S(2)}) %collective-permute-start.37) | collective-permute-done | bytes 6176 | tf_op jit(solution)/shard_map/ppermute | solution.py:35
  44.8 5.7 %collective-permute-done.38 = bf16[3072]{0:T(1024)(128)(2,1)S(1)} collective-permute-done((bf16[3072]{0:T(1024)(128)(2,1)S(1)}, bf16[3072]{0:T(1024)(128)(2,1)S(1)}, u32[]{:S(2)}, u32[]{:S(2)}) %collective-permute-start.38) | collective-permute-done | bytes 6176 | tf_op jit(solution)/shard_map/ppermute | solution.py:35
  52.5 4.1 %collective-permute-done.refs_1_ = bf16[96,1152]{1,0:T(8,128)(2,1)S(1)} collective-permute-done((bf16[96,1152]{1,0:T(8,128)(2,1)}, bf16[96,1152]{1,0:T(8,128)(2,1)S(1)}, u32[]{:S(2)}, u32[]{:S(2)}) %collective-permute-start) | collective-permute-done | bytes 221216 | tf_op jit(solution)/shard_map/ppermute | solution.py:35
  56.7 4.3 %collective-permute-start.39 = (bf16[3072]{0:T(1024)(128)(2,1)S(1)}, bf16[3072]{0:T(1024)(128)(2,1)S(1)}, u32[]{:S(2)}, u32[]{:S(2)}) collective-permute-start(bf16[3072]{0:T(1024)(128)(2,1)S(1)} %add.51), channel_id=1, source_target_pairs={{0,128},{32,160},{64,192},{96,224},{128,0},{160,32},{192,64},{224,... | collective-permute-start | bytes 18440 | tf_op jit(solution)/shard_map/ppermute | solution.py:35
  64.3 3.0 %collective-permute-start.7 = (bf16[384,1152]{1,0:T(8,128)(2,1)}, bf16[384,1152]{1,0:T(8,128)(2,1)}, u32[]{:S(2)}, u32[]{:S(2)}) collective-permute-start(bf16[384,1152]{1,0:T(8,128)(2,1)} %shard_map.139.refs_0_), channel_id=1, source_target_pairs={{0,224},{32,0},{64,32},{96,64},{128,96},{160,128},{192,160},{224,1... | collective-permute-start | bytes 2654216 | tf_op jit(solution)/shard_map/ppermute | solution.py:35
  67.3 3.2 %collective-permute-start.16 = (bf16[96,1920]{1,0:T(8,128)(2,1)}, bf16[96,1920]{1,0:T(8,128)(2,1)S(1)}, u32[]{:S(2)}, u32[]{:S(2)}) collective-permute-start(bf16[96,1920]{1,0:T(8,128)(2,1)} %collective-permute-done.15.refs_1_), channel_id=1, source_target_pairs={{0,224},{32,0},{64,32},{96,64},{128,96},{160,128},{192,160},{224,1... | collective-permute-start | bytes 1105928 | tf_op jit(solution)/shard_map/ppermute | solution.py:35
  70.5 2.9 %collective-permute-start.30 = (bf16[96,1920]{1,0:T(8,128)(2,1)}, bf16[96,1920]{1,0:T(8,128)(2,1)S(1)}, u32[]{:S(2)}, u32[]{:S(2)}) collective-permute-start(bf16[96,1920]{1,0:T(8,128)(2,1)} %get-tuple-element.34.refs_0_), channel_id=1, source_target_pairs={{0,24},{8,0},{16,8},{24,16},{1,25},{9,1},{17,9},{25,17},{2,26},{10... | collective-permute-start | bytes 1105928 | tf_op jit(solution)/shard_map/ppermute | solution.py:35
  75.4 12.3 %collective-permute-done.13.refs_0_ = bf16[96,1920]{1,0:T(8,128)(2,1)S(1)} collective-permute-done((bf16[96,1920]{1,0:T(8,128)(2,1)S(1)}, bf16[96,1920]{1,0:T(8,128)(2,1)S(1)}, u32[]{:S(2)}, u32[]{:S(2)}) %collective-permute-start.13) | collective-permute-done | bytes 368672 | tf_op jit(solution)/shard_map/ppermute | solution.py:35
  87.7 2.6 %collective-permute-start.27 = (bf16[192,1920]{1,0:T(8,128)(2,1)}, bf16[192,1920]{1,0:T(8,128)(2,1)}, u32[]{:S(2)}, u32[]{:S(2)}) collective-permute-start(bf16[192,1920]{1,0:T(8,128)(2,1)} %shard_map.142.refs_0_), channel_id=1, source_target_pairs={{0,24},{8,0},{16,8},{24,16},{1,25},{9,1},{17,9},{25,17},{2,26},{10... | collective-permute-start | bytes 2211848 | tf_op jit(solution)/shard_map/ppermute | solution.py:35
  90.5 3.3 %collective-permute-start.18 = (bf16[48,1920]{1,0:T(8,128)(2,1)S(1)}, bf16[48,1920]{1,0:T(8,128)(2,1)S(1)}, u32[]{:S(2)}, u32[]{:S(2)}) collective-permute-start(bf16[48,1920]{1,0:T(8,128)(2,1)S(1)} %slice.27), channel_id=1, source_target_pairs={{0,224},{32,0},{64,32},{96,64},{128,96},{160,128},{192,160},{224,1... | collective-permute-start | bytes 552968 | tf_op jit(solution)/shard_map/ppermute | solution.py:35
  93.8 5.4 %collective-permute-done.17.refs_2_ = bf16[48,1920]{1,0:T(8,128)(2,1)S(1)} collective-permute-done((bf16[48,1920]{1,0:T(8,128)(2,1)S(1)}, bf16[48,1920]{1,0:T(8,128)(2,1)S(1)}, u32[]{:S(2)}, u32[]{:S(2)}) %collective-permute-start.17) | collective-permute-done | bytes 184352 | tf_op jit(solution)/shard_map/ppermute | solution.py:35
  100.1 3.2 %collective-permute-start.8 = (bf16[384,1152]{1,0:T(8,128)(2,1)}, bf16[384,1152]{1,0:T(8,128)(2,1)}, u32[]{:S(2)}, u32[]{:S(2)}) collective-permute-start(bf16[384,1152]{1,0:T(8,128)(2,1)} %collective-permute-done.7.refs_1_), channel_id=1, source_target_pairs={{0,224},{32,0},{64,32},{96,64},{128,96},{160,128},{192,160},{224,1... | collective-permute-start | bytes 2654216 | tf_op jit(solution)/shard_map/ppermute | solution.py:35
  105.7 20.3 %collective-permute-done.31.refs_3_ = bf16[96,1920]{1,0:T(8,128)(2,1)S(1)} collective-permute-done((bf16[96,1920]{1,0:T(8,128)(2,1)S(1)}, bf16[96,1920]{1,0:T(8,128)(2,1)S(1)}, u32[]{:S(2)}, u32[]{:S(2)}) %collective-permute-start.31) | collective-permute-done | bytes 368672 | tf_op jit(solution)/shard_map/ppermute | solution.py:35
  130.9 3.2 %collective-permute-start.9 = (bf16[384,1152]{1,0:T(8,128)(2,1)}, bf16[384,1152]{1,0:T(8,128)(2,1)}, u32[]{:S(2)}, u32[]{:S(2)}) collective-permute-start(bf16[384,1152]{1,0:T(8,128)(2,1)} %collective-permute-done.8.refs_1_), channel_id=1, source_target_pairs={{0,224},{32,0},{64,32},{96,64},{128,96},{160,128},{192,160},{224,1... | collective-permute-start | bytes 2654216 | tf_op jit(solution)/shard_map/ppermute | solution.py:35
  134.1 30.7 %collective-permute-done.23.refs_1_ = bf16[192,1920]{1,0:T(8,128)(2,1)} collective-permute-done((bf16[192,1920]{1,0:T(8,128)(2,1)}, bf16[192,1920]{1,0:T(8,128)(2,1)}, u32[]{:S(2)}, u32[]{:S(2)}) %collective-permute-start.23) | collective-permute-done | bytes 737312 | tf_op jit(solution)/shard_map/ppermute | solution.py:35
  173.5 2.8 %shard_map.143 = (bf16[1024,3072]{1,0:T(8,128)(2,1)}, bf16[1024,3072]{1,0:T(8,128)(2,1)}, bf16[3072,1024]{1,0:T(8,128)(2,1)}) custom-call(bf16[384,1152]{1,0:T(8,128)(2,1)} %shard_map.139.refs_0_), custom_call_target="tpu_custom_call" | custom-call | flops 353894400 | bytes 1769472 | tf_op jit(solution)/shard_map/pallas_call | solution.py:171
  176.3 2.9 %shard_map.144 = (bf16[1024,3072]{1,0:T(8,128)(2,1)}, bf16[1024,3072]{1,0:T(8,128)(2,1)}, bf16[3072,1024]{1,0:T(8,128)(2,1)}) custom-call(bf16[96,1920]{1,0:T(8,128)(2,1)} %get-tuple-element.34.refs_0_, bf16[96,1920]{1,0:T(8,128)(2,1)} %copy-done.8, bf16[96,1920]{1,0:T(8,128)(2,1)} %copy-done.9, ...), custom_call_target="tpu_custom_call", output_to_operand_aliasing={{0}: (4, {}), {1}: (5, {}), {2}: (6, {})} | custom-call | flops 589824000 | bytes 2949120 | tf_op jit(solution)/shard_map/pallas_call | solution.py:171
  179.2 3.6 %shard_map.145 = (bf16[1024,3072]{1,0:T(8,128)(2,1)}, bf16[1024,3072]{1,0:T(8,128)(2,1)}, bf16[3072,1024]{1,0:T(8,128)(2,1)}) custom-call(bf16[384,1152]{1,0:T(8,128)(2,1)} %copy-done.3, bf16[384,1152]{1,0:T(8,128)(2,1)} %collective-permute-done.7.refs_1_, ...), custom_call_target="tpu_custom_call", output_to_operand_aliasing={{0}: (2, {}), {1}: (3, {}), {2}: (4, {})} | custom-call | flops 707788800 | bytes 3538944 | tf_op jit(solution)/shard_map/pallas_call | solution.py:171
  186.0 3.5 %shard_map.146 = (bf16[1024,3072]{1,0:T(8,128)(2,1)}, bf16[1024,3072]{1,0:T(8,128)(2,1)}, bf16[3072,1024]{1,0:T(8,128)(2,1)}) custom-call(bf16[192,1920]{1,0:T(8,128)(2,1)} %shard_map.142.refs_0_, bf16[192,1920]{1,0:T(8,128)(2,1)} %collective-permute-done.26.refs_1_, ...), custom_call_target="tpu_custom_call", output_to_operand_aliasing={{0}: (4, {}), {1}: (5, {}), {2}: (6, {})} | custom-call | flops 1179648000 | bytes 5898240 | tf_op jit(solution)/shard_map/pallas_call | solution.py:171
  189.5 3.6 %shard_map.147 = (bf16[1024,3072]{1,0:T(8,128)(2,1)}, bf16[1024,3072]{1,0:T(8,128)(2,1)}, bf16[3072,1024]{1,0:T(8,128)(2,1)}) custom-call(bf16[384,1152]{1,0:T(8,128)(2,1)} %collective-permute-done.4.refs_0_, bf16[384,1152]{1,0:T(8,128)(2,1)} %collective-permute-done.8.refs_1_, ...), custom_call_target="tpu_custom_call", output_to_operand_aliasing={{0}: (2, {}), {1}: (3, {}), {2}: (4, {})} | custom-call | flops 707788800 | bytes 3538944 | tf_op jit(solution)/shard_map/pallas_call | solution.py:171
  193.1 3.5 %shard_map.148 = (bf16[1024,3072]{1,0:T(8,128)(2,1)}, bf16[1024,3072]{1,0:T(8,128)(2,1)}, bf16[3072,1024]{1,0:T(8,128)(2,1)}) custom-call(bf16[192,1920]{1,0:T(8,128)(2,1)} %shard_map.141.refs_0_, bf16[192,1920]{1,0:T(8,128)(2,1)} %collective-permute-done.23.refs_1_, ...), custom_call_target="tpu_custom_call", output_to_operand_aliasing={{0}: (4, {}), {1}: (5, {}), {2}: (6, {})} | custom-call | flops 1179648000 | bytes 5898240 | tf_op jit(solution)/shard_map/pallas_call | solution.py:171
  196.7 3.6 %shard_map.149 = (bf16[1024,3072]{1,0:T(8,128)(2,1)}, bf16[1024,3072]{1,0:T(8,128)(2,1)}, bf16[3072,1024]{1,0:T(8,128)(2,1)}) custom-call(bf16[384,1152]{1,0:T(8,128)(2,1)} %copy-done.2, bf16[384,1152]{1,0:T(8,128)(2,1)} %collective-permute-done.9.refs_1_, ...), custom_call_target="tpu_custom_call", output_to_operand_aliasing={{0}: (2, {}), {1}: (3, {}), {2}: (4, {})} | custom-call | flops 707788800 | bytes 3538944 | tf_op jit(solution)/shard_map/pallas_call | solution.py:171
  200.3 4.2 %shard_map.150 = (bf16[1024,3072]{1,0:T(8,128)(2,1)}, bf16[1024,3072]{1,0:T(8,128)(2,1)}, bf16[3072,1024]{1,0:T(8,128)(2,1)}) custom-call(bf16[288,1920]{1,0:T(8,128)(2,1)} %shard_map.140.refs_0_, bf16[288,1920]{1,0:T(8,128)(2,1)} %copy-done, bf16[288,1920]{1,0:T(8,128)(2,1)} %copy-done.1, ...), custom_call_target="tpu_custom_call", output_to_operand_aliasing={{0}: (5, {}), {1}: (6, {}), {2}: (7, {})} | custom-call | flops 1769472000 | bytes 8847360 | tf_op jit(solution)/shard_map/pallas_call | solution.py:171
  205.5 2.8 %shard_map.151 = (bf16[1024,3072]{1,0:T(8,128)(2,1)}, bf16[1024,3072]{1,0:T(8,128)(2,1)}, bf16[3072,1024]{1,0:T(8,128)(2,1)}) custom-call(bf16[192,1152]{1,0:T(8,128)(2,1)} %copy-done.7, bf16[192,1152]{1,0:T(8,128)(2,1)} %copy-done.6, bf16[1024,3072]{1,0:T(8,128)(2,1)} %get-tuple-element.56.refs_2_, ...), custom_call_target="tpu_custom_call", output_to_operand_aliasing={{0}: (2, {}), {1}: (3, {}), {2}: (4, {})} | custom-call | flops 353894400 | bytes 1769472 | tf_op jit(solution)/shard_map/pallas_call | solution.py:171
  (118 shorter events, 40.7 us)
Async XLA Ops:
  3.0 14.6 %collective-permute-start.11 = (bf16[96,1920]{1,0:T(8,128)(2,1)}, bf16[96,1920]{1,0:T(8,128)(2,1)S(1)}, u32[]{:S(2)}, u32[]{:S(2)}) collective-permute-start(bf16[96,1920]{1,0:T(8,128)(2,1)} %get-tuple-element.34.refs_0_), channel_id=1, source_target_pairs={{0,32},{32,64},{64,96},{96,128},{128,160},{160,192},{192,224},{224... | collective-permute-start | bytes 1105928 | tf_op jit(solution)/shard_map/ppermute | solution.py:35
  4.9 12.7 %collective-permute-start.14 = (bf16[96,1920]{1,0:T(8,128)(2,1)}, bf16[96,1920]{1,0:T(8,128)(2,1)S(1)}, u32[]{:S(2)}, u32[]{:S(2)}) collective-permute-start(bf16[96,1920]{1,0:T(8,128)(2,1)} %get-tuple-element.34.refs_0_), channel_id=1, source_target_pairs={{0,224},{32,0},{64,32},{96,64},{128,96},{160,128},{192,160},{224,1... | collective-permute-start | bytes 1105928 | tf_op jit(solution)/shard_map/ppermute | solution.py:35
  9.7 11.1 %collective-permute-start.32 = (bf16[3072]{0:T(1024)(128)(2,1)S(1)}, bf16[3072]{0:T(1024)(128)(2,1)S(1)}, u32[]{:S(2)}, u32[]{:S(2)}) collective-permute-start(bf16[3072]{0:T(1024)(128)(2,1)S(1)} %dynamic_update_slice.5), channel_id=1, source_target_pairs={{0,1},{1,0},{2,3},{3,2},{4,5},{5,4},{6,7},{7,6},{8,9},{9,8},{10,11... | collective-permute-start | bytes 18440 | tf_op jit(solution)/shard_map/ppermute | solution.py:35
  9.8 60.7 %collective-permute-start.29 = (bf16[96,1920]{1,0:T(8,128)(2,1)}, bf16[96,1920]{1,0:T(8,128)(2,1)S(1)}, u32[]{:S(2)}, u32[]{:S(2)}) collective-permute-start(bf16[96,1920]{1,0:T(8,128)(2,1)} %get-tuple-element.34.refs_0_), channel_id=1, source_target_pairs={{0,8},{8,16},{16,24},{24,0},{1,9},{9,17},{17,25},{25,1},{2,10},{10... | collective-permute-start | bytes 1105928 | tf_op jit(solution)/shard_map/ppermute | solution.py:35
  11.4 40.7 %collective-permute-start.1 = (bf16[96,1152]{1,0:T(8,128)(2,1)}, bf16[96,1152]{1,0:T(8,128)(2,1)S(1)}, u32[]{:S(2)}, u32[]{:S(2)}) collective-permute-start(bf16[96,1152]{1,0:T(8,128)(2,1)} %get-tuple-element.33.refs_0_), channel_id=1, source_target_pairs={{0,24},{8,0},{16,8},{24,16},{1,25},{9,1},{17,9},{25,17},{2,26},{10... | collective-permute-start | bytes 663560 | tf_op jit(solution)/shard_map/ppermute | solution.py:35
  17.6 49.6 %collective-permute-start.12 = (bf16[96,1920]{1,0:T(8,128)(2,1)S(1)}, bf16[96,1920]{1,0:T(8,128)(2,1)S(1)}, u32[]{:S(2)}, u32[]{:S(2)}) collective-permute-start(bf16[96,1920]{1,0:T(8,128)(2,1)S(1)} %collective-permute-done.11.refs_0_), channel_id=1, source_target_pairs={{0,32},{32,64},{64,96},{96,128},{128,160},{160,192},{192,224},{224... | collective-permute-start | bytes 1105928 | tf_op jit(solution)/shard_map/ppermute | solution.py:35
  17.6 49.6 %collective-permute-start.15 = (bf16[96,1920]{1,0:T(8,128)(2,1)S(1)}, bf16[96,1920]{1,0:T(8,128)(2,1)}, u32[]{:S(2)}, u32[]{:S(2)}) collective-permute-start(bf16[96,1920]{1,0:T(8,128)(2,1)S(1)} %collective-permute-done.14.refs_1_), channel_id=1, source_target_pairs={{0,224},{32,0},{64,32},{96,64},{128,96},{160,128},{192,160},{224,1... | collective-permute-start | bytes 1105928 | tf_op jit(solution)/shard_map/ppermute | solution.py:35
  52.1 8.8 %collective-permute-start.2 = (bf16[96,1152]{1,0:T(8,128)(2,1)S(1)}, bf16[96,1152]{1,0:T(8,128)(2,1)S(1)}, u32[]{:S(2)}, u32[]{:S(2)}) collective-permute-start(bf16[96,1152]{1,0:T(8,128)(2,1)S(1)} %collective-permute-done.1.refs_2_), channel_id=1, source_target_pairs={{0,24},{8,0},{16,8},{24,16},{1,25},{9,1},{17,9},{25,17},{2,26},{10... | collective-permute-start | bytes 663560 | tf_op jit(solution)/shard_map/ppermute | solution.py:35
  63.9 36.2 %collective-permute-start.3 = (bf16[384,1152]{1,0:T(8,128)(2,1)}, bf16[384,1152]{1,0:T(8,128)(2,1)S(1)}, u32[]{:S(2)}, u32[]{:S(2)}) collective-permute-start(bf16[384,1152]{1,0:T(8,128)(2,1)} %shard_map.139.refs_0_), channel_id=1, source_target_pairs={{0,32},{32,64},{64,96},{96,128},{128,160},{160,192},{192,224},{224... | collective-permute-start | bytes 2654216 | tf_op jit(solution)/shard_map/ppermute | solution.py:35
  64.3 35.9 %collective-permute-start.7 = (bf16[384,1152]{1,0:T(8,128)(2,1)}, bf16[384,1152]{1,0:T(8,128)(2,1)}, u32[]{:S(2)}, u32[]{:S(2)}) collective-permute-start(bf16[384,1152]{1,0:T(8,128)(2,1)} %shard_map.139.refs_0_), channel_id=1, source_target_pairs={{0,224},{32,0},{64,32},{96,64},{128,96},{160,128},{192,160},{224,1... | collective-permute-start | bytes 2654216 | tf_op jit(solution)/shard_map/ppermute | solution.py:35
  67.2 20.4 %collective-permute-start.13 = (bf16[96,1920]{1,0:T(8,128)(2,1)S(1)}, bf16[96,1920]{1,0:T(8,128)(2,1)S(1)}, u32[]{:S(2)}, u32[]{:S(2)}) collective-permute-start(bf16[96,1920]{1,0:T(8,128)(2,1)S(1)} %collective-permute-done.12.refs_0_), channel_id=1, source_target_pairs={{0,32},{32,64},{64,96},{96,128},{128,160},{160,192},{192,224},{224... | collective-permute-start | bytes 1105928 | tf_op jit(solution)/shard_map/ppermute | solution.py:35
  67.3 23.1 %collective-permute-start.16 = (bf16[96,1920]{1,0:T(8,128)(2,1)}, bf16[96,1920]{1,0:T(8,128)(2,1)S(1)}, u32[]{:S(2)}, u32[]{:S(2)}) collective-permute-start(bf16[96,1920]{1,0:T(8,128)(2,1)} %collective-permute-done.15.refs_1_), channel_id=1, source_target_pairs={{0,224},{32,0},{64,32},{96,64},{128,96},{160,128},{192,160},{224,1... | collective-permute-start | bytes 1105928 | tf_op jit(solution)/shard_map/ppermute | solution.py:35
  70.5 20.0 %collective-permute-start.30 = (bf16[96,1920]{1,0:T(8,128)(2,1)}, bf16[96,1920]{1,0:T(8,128)(2,1)S(1)}, u32[]{:S(2)}, u32[]{:S(2)}) collective-permute-start(bf16[96,1920]{1,0:T(8,128)(2,1)} %get-tuple-element.34.refs_0_), channel_id=1, source_target_pairs={{0,24},{8,0},{16,8},{24,16},{1,25},{9,1},{17,9},{25,17},{2,26},{10... | collective-permute-start | bytes 1105928 | tf_op jit(solution)/shard_map/ppermute | solution.py:35
  87.7 39.0 %collective-permute-start.27 = (bf16[192,1920]{1,0:T(8,128)(2,1)}, bf16[192,1920]{1,0:T(8,128)(2,1)}, u32[]{:S(2)}, u32[]{:S(2)}) collective-permute-start(bf16[192,1920]{1,0:T(8,128)(2,1)} %shard_map.142.refs_0_), channel_id=1, source_target_pairs={{0,24},{8,0},{16,8},{24,16},{1,25},{9,1},{17,9},{25,17},{2,26},{10... | collective-permute-start | bytes 2211848 | tf_op jit(solution)/shard_map/ppermute | solution.py:35
  90.3 8.8 %collective-permute-start.17 = (bf16[48,1920]{1,0:T(8,128)(2,1)S(1)}, bf16[48,1920]{1,0:T(8,128)(2,1)S(1)}, u32[]{:S(2)}, u32[]{:S(2)}) collective-permute-start(bf16[48,1920]{1,0:T(8,128)(2,1)S(1)} %slice.26), channel_id=1, source_target_pairs={{0,32},{32,64},{64,96},{96,128},{128,160},{160,192},{192,224},{224... | collective-permute-start | bytes 552968 | tf_op jit(solution)/shard_map/ppermute | solution.py:35
  90.5 8.7 %collective-permute-start.18 = (bf16[48,1920]{1,0:T(8,128)(2,1)S(1)}, bf16[48,1920]{1,0:T(8,128)(2,1)S(1)}, u32[]{:S(2)}, u32[]{:S(2)}) collective-permute-start(bf16[48,1920]{1,0:T(8,128)(2,1)S(1)} %slice.27), channel_id=1, source_target_pairs={{0,224},{32,0},{64,32},{96,64},{128,96},{160,128},{192,160},{224,1... | collective-permute-start | bytes 552968 | tf_op jit(solution)/shard_map/ppermute | solution.py:35
  99.1 31.0 %collective-permute-start.26 = (bf16[192,1920]{1,0:T(8,128)(2,1)}, bf16[192,1920]{1,0:T(8,128)(2,1)}, u32[]{:S(2)}, u32[]{:S(2)}) collective-permute-start(bf16[192,1920]{1,0:T(8,128)(2,1)} %shard_map.142.refs_0_), channel_id=1, source_target_pairs={{0,8},{8,16},{16,24},{24,0},{1,9},{9,17},{17,25},{25,1},{2,10},{10... | collective-permute-start | bytes 2211848 | tf_op jit(solution)/shard_map/ppermute | solution.py:35
  99.2 26.8 %collective-permute-start.31 = (bf16[96,1920]{1,0:T(8,128)(2,1)S(1)}, bf16[96,1920]{1,0:T(8,128)(2,1)S(1)}, u32[]{:S(2)}, u32[]{:S(2)}) collective-permute-start(bf16[96,1920]{1,0:T(8,128)(2,1)S(1)} %collective-permute-done.29.refs_1_), channel_id=1, source_target_pairs={{0,8},{8,16},{16,24},{24,0},{1,9},{9,17},{17,25},{25,1},{2,10},{10... | collective-permute-start | bytes 1105928 | tf_op jit(solution)/shard_map/ppermute | solution.py:35
  100.1 30.8 %collective-permute-start.4 = (bf16[384,1152]{1,0:T(8,128)(2,1)S(1)}, bf16[384,1152]{1,0:T(8,128)(2,1)}, u32[]{:S(2)}, u32[]{:S(2)}) collective-permute-start(bf16[384,1152]{1,0:T(8,128)(2,1)S(1)} %collective-permute-done.3.refs_0_), channel_id=1, source_target_pairs={{0,32},{32,64},{64,96},{96,128},{128,160},{160,192},{192,224},{224... | collective-permute-start | bytes 2654216 | tf_op jit(solution)/shard_map/ppermute | solution.py:35
  100.1 30.8 %collective-permute-start.8 = (bf16[384,1152]{1,0:T(8,128)(2,1)}, bf16[384,1152]{1,0:T(8,128)(2,1)}, u32[]{:S(2)}, u32[]{:S(2)}) collective-permute-start(bf16[384,1152]{1,0:T(8,128)(2,1)} %collective-permute-done.7.refs_1_), channel_id=1, source_target_pairs={{0,224},{32,0},{64,32},{96,64},{128,96},{160,128},{192,160},{224,1... | collective-permute-start | bytes 2654216 | tf_op jit(solution)/shard_map/ppermute | solution.py:35
  126.0 41.1 %collective-permute-start.19 = (bf16[288,1920]{1,0:T(8,128)(2,1)}, bf16[288,1920]{1,0:T(8,128)(2,1)S(1)}, u32[]{:S(2)}, u32[]{:S(2)}) collective-permute-start(bf16[288,1920]{1,0:T(8,128)(2,1)} %shard_map.140.refs_0_), channel_id=1, source_target_pairs={{0,8},{8,16},{16,24},{24,0},{1,9},{9,17},{17,25},{25,1},{2,10},{10... | collective-permute-start | bytes 3317768 | tf_op jit(solution)/shard_map/ppermute | solution.py:35
  126.7 40.5 %collective-permute-start.20 = (bf16[288,1920]{1,0:T(8,128)(2,1)}, bf16[288,1920]{1,0:T(8,128)(2,1)S(1)}, u32[]{:S(2)}, u32[]{:S(2)}) collective-permute-start(bf16[288,1920]{1,0:T(8,128)(2,1)} %shard_map.140.refs_0_), channel_id=1, source_target_pairs={{0,24},{8,0},{16,8},{24,16},{1,25},{9,1},{17,9},{25,17},{2,26},{10... | collective-permute-start | bytes 3317768 | tf_op jit(solution)/shard_map/ppermute | solution.py:35
  130.2 34.7 %collective-permute-start.23 = (bf16[192,1920]{1,0:T(8,128)(2,1)}, bf16[192,1920]{1,0:T(8,128)(2,1)}, u32[]{:S(2)}, u32[]{:S(2)}) collective-permute-start(bf16[192,1920]{1,0:T(8,128)(2,1)} %shard_map.141.refs_0_), channel_id=1, source_target_pairs={{0,8},{8,16},{16,24},{24,0},{1,9},{9,17},{17,25},{25,1},{2,10},{10... | collective-permute-start | bytes 2211848 | tf_op jit(solution)/shard_map/ppermute | solution.py:35
  130.9 40.0 %collective-permute-start.5 = (bf16[384,1152]{1,0:T(8,128)(2,1)}, bf16[384,1152]{1,0:T(8,128)(2,1)S(1)}, u32[]{:S(2)}, u32[]{:S(2)}) collective-permute-start(bf16[384,1152]{1,0:T(8,128)(2,1)} %collective-permute-done.4.refs_0_), channel_id=1, source_target_pairs={{0,32},{32,64},{64,96},{96,128},{128,160},{160,192},{192,224},{224... | collective-permute-start | bytes 2654216 | tf_op jit(solution)/shard_map/ppermute | solution.py:35
  130.9 40.0 %collective-permute-start.9 = (bf16[384,1152]{1,0:T(8,128)(2,1)}, bf16[384,1152]{1,0:T(8,128)(2,1)}, u32[]{:S(2)}, u32[]{:S(2)}) collective-permute-start(bf16[384,1152]{1,0:T(8,128)(2,1)} %collective-permute-done.8.refs_1_), channel_id=1, source_target_pairs={{0,224},{32,0},{64,32},{96,64},{128,96},{160,128},{192,160},{224,1... | collective-permute-start | bytes 2654216 | tf_op jit(solution)/shard_map/ppermute | solution.py:35
  164.9 19.0 %collective-permute-start.24 = (bf16[192,1920]{1,0:T(8,128)(2,1)}, bf16[192,1920]{1,0:T(8,128)(2,1)}, u32[]{:S(2)}, u32[]{:S(2)}) collective-permute-start(bf16[192,1920]{1,0:T(8,128)(2,1)} %shard_map.141.refs_0_), channel_id=1, source_target_pairs={{0,24},{8,0},{16,8},{24,16},{1,25},{9,1},{17,9},{25,17},{2,26},{10... | collective-permute-start | bytes 2211848 | tf_op jit(solution)/shard_map/ppermute | solution.py:35
  167.1 17.7 %collective-permute-start.28 = (bf16[192,1920]{1,0:T(8,128)(2,1)}, bf16[192,1920]{1,0:T(8,128)(2,1)}, u32[]{:S(2)}, u32[]{:S(2)}) collective-permute-start(bf16[192,1920]{1,0:T(8,128)(2,1)} %collective-permute-done.27.refs_2_), channel_id=1, source_target_pairs={{0,24},{8,0},{16,8},{24,16},{1,25},{9,1},{17,9},{25,17},{2,26},{10... | collective-permute-start | bytes 2211848 | tf_op jit(solution)/shard_map/ppermute | solution.py:35
  167.2 25.9 %collective-permute-start.25 = (bf16[192,1920]{1,0:T(8,128)(2,1)}, bf16[192,1920]{1,0:T(8,128)(2,1)}, u32[]{:S(2)}, u32[]{:S(2)}) collective-permute-start(bf16[192,1920]{1,0:T(8,128)(2,1)} %collective-permute-done.23.refs_1_), channel_id=1, source_target_pairs={{0,8},{8,16},{16,24},{24,0},{1,9},{9,17},{17,25},{25,1},{2,10},{10... | collective-permute-start | bytes 2211848 | tf_op jit(solution)/shard_map/ppermute | solution.py:35
  170.9 29.4 %collective-permute-start.21 = (bf16[144,1920]{1,0:T(8,128)(2,1)}, bf16[144,1920]{1,0:T(8,128)(2,1)}, u32[]{:S(2)}, u32[]{:S(2)}) collective-permute-start(bf16[144,1920]{1,0:T(8,128)(2,1)} %slice.28), channel_id=1, source_target_pairs={{0,8},{8,16},{16,24},{24,0},{1,9},{9,17},{17,25},{25,1},{2,10},{10... | collective-permute-start | bytes 1658888 | tf_op jit(solution)/shard_map/ppermute | solution.py:35
  170.9 29.3 %collective-permute-start.22 = (bf16[144,1920]{1,0:T(8,128)(2,1)}, bf16[144,1920]{1,0:T(8,128)(2,1)}, u32[]{:S(2)}, u32[]{:S(2)}) collective-permute-start(bf16[144,1920]{1,0:T(8,128)(2,1)} %slice.29), channel_id=1, source_target_pairs={{0,24},{8,0},{16,8},{24,16},{1,25},{9,1},{17,9},{25,17},{2,26},{10... | collective-permute-start | bytes 1658888 | tf_op jit(solution)/shard_map/ppermute | solution.py:35
  183.9 20.6 %collective-permute-start.10 = (bf16[192,1152]{1,0:T(8,128)(2,1)S(1)}, bf16[192,1152]{1,0:T(8,128)(2,1)S(1)}, u32[]{:S(2)}, u32[]{:S(2)}) collective-permute-start(bf16[192,1152]{1,0:T(8,128)(2,1)S(1)} %slice.25), channel_id=1, source_target_pairs={{0,224},{32,0},{64,32},{96,64},{128,96},{160,128},{192,160},{224,1... | collective-permute-start | bytes 1327112 | tf_op jit(solution)/shard_map/ppermute | solution.py:35
  184.8 19.7 %collective-permute-start.6 = (bf16[192,1152]{1,0:T(8,128)(2,1)S(1)}, bf16[192,1152]{1,0:T(8,128)(2,1)S(1)}, u32[]{:S(2)}, u32[]{:S(2)}) collective-permute-start(bf16[192,1152]{1,0:T(8,128)(2,1)S(1)} %slice.24), channel_id=1, source_target_pairs={{0,32},{32,64},{64,96},{96,128},{128,160},{160,192},{192,224},{224... | collective-permute-start | bytes 1327112 | tf_op jit(solution)/shard_map/ppermute | solution.py:35
  (27 other events, 455.7 us)
where the time goes:
time: 209 us; the launch traced here: 208 us
  waiting for transfers between devices  101 us (48%)
  starting transfers between devices  57.8 us (28%)
  Pallas kernels  41.3 us (20%)
  local copies, waits for them, and re-layouts  5.68 us (3%)
    ppermute x40, waiting for transfers between devices, shifted(): return lax.ppermute(x, axis, [(i, (i + step) % n) for i in range(n)])  101 us
    ppermute x40, starting transfers between devices, shifted(): return lax.ppermute(x, axis, [(i, (i + step) % n) for i in range(n)])  57.8 us
    pallas_call x9, Pallas kernels, placed(): pl.pallas_call(functools.partial(place_body, first, kind, blocks, len(src...  30.4 us
    pallas_call x4, Pallas kernels, stacked(): pl.pallas_call(functools.partial(stack_body, starts), out_shape=jax.Shape...  8.58 us
  transfers between devices with their start and end apart: 40, of which 13 were waited for; matrix products, arithmetic and copies ran while one was open for 2% of the time, Pallas kernels for 17%

commit v1 on v0

v1 whole, which is shorter than its diff:
```python
import functools

import jax
import jax.numpy as jnp
from jax import lax
from jax.experimental import pallas as pl
from jax.experimental.pallas import tpu as pltpu
from jax.sharding import Mesh
from jax.sharding import PartitionSpec as P


ZERO = ("zero_0", "zero_1")
ZERO_TP = ("zero_0", "zero_1", "tp_0", "tp_1")
TP = ("tp_0", "tp_1")
NZ, NY = 8, 4
D_MODEL, D_INNER, RANK = 3072, 8192, 16


mix_rate = 0.5

ROWS = 96
BLOCK = NY * ROWS
WIDE = 1024
CUT = 128
A_COLS = WIDE + CUT
B_COLS = WIDE + WIDE - CUT
STEP = 128
UP = 192
GRANT = 1 << 20

ANY = pl.BlockSpec(memory_space=pl.ANY)
VMEM = pl.BlockSpec(memory_space=pltpu.VMEM)
HBM = pl.BlockSpec(memory_space=pltpu.HBM)


SIZES = {"zero_0": NZ, "zero_1": NY, "tp_0": 4, "tp_1": 2}


def shifted(x, axis, step):
    n = SIZES[axis]
    return lax.ppermute(x, axis, [(i, (i + step) % n) for i in range(n)])


def merged(train, low, high):
    product = lax.dot_general(
        low, high, (((0,), (0,)), ((), ())), preferred_element_type=jnp.float32
    )
    return (train.astype(jnp.float32) + mix_rate * product).astype(jnp.bfloat16)


def merge_body(*refs):
    ins, (out_all, out_b), held, sems = refs[:9], refs[9:11], refs[11:20], refs[20]
    loads = [
        pltpu.make_async_copy(src, dst, sems.at[k])
        for k, (src, dst) in enumerate(zip(ins, held, strict=True))
    ]
    for c in loads:
        c.start()
    for c in loads:
        c.wait()
    tg, lg, hg, td, ld, hd, tu, lu, hu = held
    up = merged(tu[...], lu[...], hu[...])
    down = merged(td[...], ld[...], hd[...])
    for out, at in ((out_b, 0), (out_all, A_COLS)):
        out[:, at : at + WIDE] = down
        out[:, at + WIDE : at + B_COLS] = up[:, CUT:]
    out_all[:, :WIDE] = merged(tg[...], lg[...], hg[...])
    if CUT:
        out_all[:, WIDE:A_COLS] = up[:, :CUT]


def merge_call(*args):
    return pl.pallas_call(
        merge_body,
        out_shape=(
            jax.ShapeDtypeStruct((ROWS, A_COLS + B_COLS), jnp.bfloat16),
            jax.ShapeDtypeStruct((ROWS, B_COLS), jnp.bfloat16),
        ),
        in_specs=[HBM] * len(args),
        out_specs=(VMEM, VMEM),
        scratch_shapes=[pltpu.VMEM(a.shape, a.dtype) for a in args]
        + [pltpu.SemaphoreType.DMA((len(args),))],
    )(*args)


def stack_body(starts, *refs):
    pieces, out, sems = refs[:-2], refs[-2], refs[-1]
    y = lax.axis_index("zero_1")
    copies = []
    for k, piece in enumerate(pieces):
        rel, row = starts[k]
        at = row if rel is None else lax.rem(y + rel, NY) * ROWS + row
        at = at if rel is None else pl.multiple_of(at, 16)
        copies.append(
            pltpu.make_async_copy(
                piece.at[:, pl.ds(0, out.shape[1])],
                out.at[pl.ds(at, piece.shape[0])],
                sems.at[k],
            )
        )
    for c in copies:
        c.start()
    for c in copies:
        c.wait()


def stacked(pieces, starts, cols=B_COLS):
    rows = sum(p.shape[0] for p in pieces)
    nbytes = rows * cols * 4
    return pl.pallas_call(
        functools.partial(stack_body, starts),
        out_shape=jax.ShapeDtypeStruct((rows, cols), jnp.bfloat16),
        in_specs=[ANY] * len(pieces),
        out_specs=VMEM,
        scratch_shapes=[pltpu.SemaphoreType.DMA((len(pieces),))],
        compiler_params=pltpu.CompilerParams(vmem_limit_bytes=nbytes + GRANT),
        cost_estimate=pl.CostEstimate(
            flops=nbytes * 100, bytes_accessed=nbytes, transcendentals=0
        ),
    )(*pieces)


def place_body(first, blocks, nsrc, *refs):
    srcs = refs[:nsrc]
    outs = refs[nsrc + (0 if first else 3) :][:3]
    held, turned, in_sem, out_sem = refs[-4:]
    gate, up, down = outs
    z, y = lax.axis_index("zero_0"), lax.axis_index("zero_1")
    taken, loads = 0, []
    for b, (kind, _, parts) in enumerate(blocks):
        mine = []
        cols = pl.ds(0, A_COLS if kind == "a" else B_COLS)
        for src, srow, rows, rel, row in parts:
            at = row
            if rel is not None:
                at = pl.multiple_of(lax.rem(y + rel, NY) * ROWS + row, 16)
            c = pltpu.make_async_copy(
                srcs[src].at[
                    pl.ds(srow, rows), pl.ds(srcs[src].shape[1] - cols.size, cols.size)
                ],
                held.at[b, pl.ds(at, rows), cols],
                in_sem.at[taken],
            )
            c.start()
            mine.append(c)
            taken += 1
        loads.append(mine)
    stores = []
    for b, (kind, zrel, _) in enumerate(blocks):
        for c in loads[b]:
            c.wait()
        zabs = lax.rem(z + zrel, NZ)
        cols = pl.ds(pl.multiple_of(zabs * BLOCK, 128), BLOCK)
        if kind == "b":
            c = pltpu.make_async_copy(
                held.at[b, :, pl.ds(0, WIDE)], down.at[cols], out_sem.at[b, 0]
            )
            c.start()
            stores.append(c)
            groups = [(WIDE, WIDE - CUT, up, CUT, 1)]
        else:
            groups = [(0, WIDE, gate, 0, 0)]
            groups += [(WIDE, CUT, up, 0, 1)] if CUT else []
        for start, width, out, row, k in groups:
            base = start if kind == "a" else start - WIDE

            def turn(i, _, start=start, base=base, b=b):
                src = pl.multiple_of(start + i * STEP, STEP)
                dst = pl.multiple_of(base + i * STEP, STEP)
                turned[b, pl.ds(dst, STEP), :] = held[b, :, pl.ds(src, STEP)].T
                return 0

            lax.fori_loop(0, width // STEP, turn, 0)
            c = pltpu.make_async_copy(
                turned.at[b, pl.ds(base, width)],
                out.at[pl.ds(row, width), cols],
                out_sem.at[b, k],
            )
            c.start()
            stores.append(c)
    for c in stores:
        c.wait()


OUT_SHAPES = (
    jax.ShapeDtypeStruct((WIDE, NZ * BLOCK), jnp.bfloat16),
    jax.ShapeDtypeStruct((WIDE, NZ * BLOCK), jnp.bfloat16),
    jax.ShapeDtypeStruct((NZ * BLOCK, WIDE), jnp.bfloat16),
)


def placed(outs, blocks, srcs):
    first = outs is None
    n = len(blocks)
    kinds = {b[0] for b in blocks}
    cols = B_COLS if "b" in kinds else A_COLS
    tall = A_COLS if "a" in kinds else WIDE - CUT
    extra = () if first else tuple(outs)
    nbytes = n * BLOCK * cols * 4
    grant = 2 * n * BLOCK * (cols + tall) + GRANT
    return pl.pallas_call(
        functools.partial(place_body, first, blocks, len(srcs)),
        out_shape=OUT_SHAPES,
        in_specs=[ANY] * len(srcs) + [HBM] * len(extra),
        out_specs=[HBM] * 3,
        input_output_aliases={}
        if first
        else {len(srcs) + k: k for k in range(3)},
        scratch_shapes=[
            pltpu.VMEM((n, BLOCK, cols), jnp.bfloat16),
            pltpu.VMEM((n, tall, BLOCK), jnp.bfloat16),
            pltpu.SemaphoreType.DMA((sum(len(b[2]) for b in blocks),)),
            pltpu.SemaphoreType.DMA((n, 2)),
        ],
        compiler_params=pltpu.CompilerParams(vmem_limit_bytes=grant),
        cost_estimate=pl.CostEstimate(
            flops=nbytes * 200, bytes_accessed=nbytes, transcendentals=0
        ),
    )(*srcs, *extra)


def per_device(
    train_gate,
    low_gate,
    high_gate,
    train_up,
    low_up,
    high_up,
    train_down,
    low_down,
    high_down,
    norm_train,
    norm_step,
):
    z, y = "zero_0", "zero_1"
    part = 112

    gain = (norm_train + norm_step).astype(jnp.bfloat16)
    place = lax.axis_index(ZERO_TP) * gain.shape[0]
    full = lax.dynamic_update_slice(
        jnp.zeros((gain.shape[0] * 256,), jnp.bfloat16), gain, (place,)
    )
    full = lax.optimization_barrier(full)

    def sent(k, full):
        axis, step = (
            (z, -1),
            (y, -1),
            (y, 2),
            ("tp_1", 1),
            ("tp_0", 1),
            (z, -2),
            ("tp_0", 2),
            (z, 4),
        )[k]
        return shifted(full, axis, step)

    def added(full, other):
        return full + other

    def b_blocks(rels, at):
        return tuple(
            (
                "b",
                rel,
                tuple(
                    (at + s, i * ROWS, ROWS, yrel, 0)
                    for s, yrel in enumerate((0, 3, 1, 2))
                ),
            )
            for i, rel in enumerate(rels)
        )

    def a_block(rel, s):
        return ("a", rel, ((s, 0, BLOCK, None, 0),))

    own, own_b = merge_call(
        train_gate,
        low_gate.T,
        high_gate,
        train_down.T,
        high_down,
        low_down.T,
        train_up,
        low_up.T,
        high_up,
    )
    l0 = shifted(own, y, 1)
    r0 = shifted(own, y, -1)
    f1 = shifted(own_b, z, 1)
    g1 = shifted(own_b, z, -1)
    o0 = shifted(l0, y, 1)
    f2 = shifted(f1, z, 1)
    g2 = shifted(g1, z, -1)
    s1 = stacked((f1, g1), ((None, 0), (None, 96)))
    r1 = shifted(s1, y, -1)
    l1 = shifted(s1, y, 1)
    n0 = sent(0, full)
    f3 = shifted(f2, z, 1)
    g3 = shifted(g2, z, -1)
    block = stacked((own, l0, r0, o0), ((0, 0), (3, 0), (1, 0), (2, 0)), A_COLS)
    p1 = shifted(block, z, 1)
    q1 = shifted(block, z, -1)
    s2 = stacked((f2, g2), ((None, 0), (None, 96)))
    full = added(full, n0)
    n1 = sent(1, full)
    r2 = shifted(s2, y, -1)
    l2 = shifted(s2, y, 1)
    outs = placed(None, (a_block(0, 0),), (block,))
    outs = placed(outs, b_blocks((0,), 0), (own, l0, r0, o0))
    f4 = shifted(f3, z, 1)
    full = added(full, n1)
    n2 = sent(2, full)
    o1 = shifted(l1, y, 1)
    o2 = shifted(r2, y, -1)
    q2 = shifted(q1, z, -1)
    p2 = shifted(p1, z, 1)
    full = added(full, n2)
    n3 = sent(3, full)
    s3 = stacked((f3, g3, f4), ((None, 0), (None, 96), (None, 192)))
    l3 = shifted(s3, y, 1)
    r3 = shifted(s3, y, -1)
    full = added(full, n3)
    n4 = sent(4, full)
    outs = placed(outs, (a_block(7, 0), a_block(1, 1)), (p1, q1))
    full = added(full, n4)
    n5 = sent(5, full)
    q3 = shifted(q2, z, -1)
    p3 = shifted(p2, z, 1)
    outs = placed(outs, b_blocks((7, 1), 0), (s1, l1, r1, o1))
    full = added(full, n5)
    n6 = sent(6, full)
    outs = placed(outs, b_blocks((6, 2), 0), (s2, l2, r2, o2))
    outs = placed(outs, (a_block(6, 0), a_block(2, 1)), (p2, q2))
    b3 = shifted(r3[part:], y, -1)
    t3 = shifted(l3[:part], y, 1)
    q4 = shifted(q3[UP:], z, -1)
    p4 = shifted(p3[:UP], z, 1)
    full = added(full, n6)
    n7 = sent(7, full)
    outs = placed(outs, (a_block(5, 0), a_block(3, 1)), (p3, q3))
    near = [[(s, i * ROWS, ROWS, r, 0) for s, r in enumerate((0, 3, 1))] for i in range(3)]
    cut = part - ROWS
    far = (
        ((3, 0, ROWS, 2, 0),),
        ((3, ROWS, cut, 2, 0), (4, 0, ROWS - cut, 2, cut)),
        ((4, ROWS - cut, ROWS, 2, 0),),
    )
    outs = placed(
        outs,
        tuple(
            ("b", rel, (*n, *f)) for rel, n, f in zip((5, 3, 4), near, far, strict=True)
        ),
        (s3, l3, r3, t3, b3),
    )
    outs = placed(
        outs, (("a", 4, ((0, 0, UP, None, 0), (1, 0, BLOCK - UP, None, UP))),), (p4, q4)
    )
    full = added(full, n7)
    return (*outs, full)


def solution(mesh):
    finer = Mesh(mesh.devices.reshape(8, 4, 4, 2), ("zero_0", "zero_1", "tp_0", "tp_1"))
    in_specs = (
        P(ZERO, TP),
        P(ZERO, None),
        P(None, TP),
        P(ZERO, TP),
        P(ZERO, None),
        P(None, TP),
        P(TP, ZERO),
        P(TP, None),
        P(None, ZERO),
        P(ZERO_TP),
        P(ZERO_TP),
    )
    out_specs = (P(TP, None), P(TP, None), P(None, TP), P())

    step = jax.shard_map(
        per_device, mesh=finer, in_specs=in_specs, out_specs=out_specs, check_vma=False
    )
    low, wide = D_MODEL, D_INNER
    shapes = ((low, wide), (low, RANK), (RANK, wide)) * 2
    shapes += ((wide, low), (wide, RANK), (RANK, low))
    jax.eval_shape(
        step,
        *(jax.ShapeDtypeStruct(s, jnp.bfloat16) for s in shapes),
        *(jax.ShapeDtypeStruct((low,), jnp.float32) for _ in range(2)),
    )
    return step
```

time: 209 us -> 221 us (1.057)
  the two profiles are of different devices: /device:TPU:8 before, /device:TPU:32 now
where the time goes in v1:
time: 221 us
  waiting for transfers between devices  110 us (50%)
  starting transfers between devices  73 us (33%)
  Pallas kernels  31.8 us (14%)
  local copies, waits for them, and re-layouts  3.42 us (2%)
    ppermute x36, waiting for transfers between devices, shifted(): return lax.ppermute(x, axis, [(i, (i + step) % n) for i in range(n)])  110 us
    ppermute x36, starting transfers between devices, shifted(): return lax.ppermute(x, axis, [(i, (i + step) % n) for i in range(n)])  73 us
    pallas_call x9, Pallas kernels, placed(): pl.pallas_call(functools.partial(place_body, first, blocks, len(srcs)), o...  26.6 us
  transfers between devices with their start and end apart: 36, of which 16 were waited for; matrix products, arithmetic and copies ran while one was open for 1% of the time, Pallas kernels for 12%

profile of v1, /device:TPU:32, one launch (start us, length us, event | category | flops | bytes accessed | tf_op | source)
XLA Modules:
  0.0 220.7 jit_solution(7694235034661782814)
XLA Ops:
  0.6 2.5 %shard_map.138 = (bf16[96,3072]{1,0:T(8,128)(2,1)}, bf16[96,1920]{1,0:T(8,128)(2,1)}) custom-call(bf16[96,1024]{1,0:T(8,128)(2,1)} %refs_0_.1, bf16[16,96]{1,0:T(8,128)(2,1)} %bitcast.6, bf16[16,1024]{1,0:T(8,128)(2,1)} %refs_2_.1, bf16[96,1024]{1,0:T(8,128)(2,1)} %bitcast.4, bf16[16,96]{1,0:T(8,128)(2,1)} %refs_4_.1, bf16[16,1024]{1,0:T(8,128)(2,1)} %bitcast.5, ...), custom_call_target="tpu_custom_call" | custom-call | tf_op jit(solution)/shard_map/pallas_call | solution.py:73
  6.5 13.3 %collective-permute-done.refs_1_ = bf16[96,3072]{1,0:T(8,128)(2,1)S(1)} collective-permute-done((bf16[96,3072]{1,0:T(8,128)(2,1)}, bf16[96,3072]{1,0:T(8,128)(2,1)S(1)}, u32[]{:S(2)}, u32[]{:S(2)}) %collective-permute-start) | collective-permute-done | bytes 589856 | tf_op jit(solution)/shard_map/ppermute | solution.py:41
  22.1 7.4 %collective-permute-done.11.refs_0_ = bf16[96,1920]{1,0:T(8,128)(2,1)S(1)} collective-permute-done((bf16[96,1920]{1,0:T(8,128)(2,1)}, bf16[96,1920]{1,0:T(8,128)(2,1)S(1)}, u32[]{:S(2)}, u32[]{:S(2)}) %collective-permute-start.11) | collective-permute-done | bytes 368672 | tf_op jit(solution)/shard_map/ppermute | solution.py:41
  31.4 2.4 %collective-permute-start.15 = (bf16[96,1920]{1,0:T(8,128)(2,1)S(1)}, bf16[96,1920]{1,0:T(8,128)(2,1)}, u32[]{:S(2)}, u32[]{:S(2)}) collective-permute-start(bf16[96,1920]{1,0:T(8,128)(2,1)S(1)} %collective-permute-done.14.refs_1_), channel_id=1, source_target_pairs={{0,224},{32,0},{64,32},{96,64},{128,96},{160,128},{192,160},{224,1... | collective-permute-start | bytes 1105928 | tf_op jit(solution)/shard_map/ppermute | solution.py:41
  38.6 4.7 %collective-permute-done.12.refs_0_ = bf16[96,1920]{1,0:T(8,128)(2,1)} collective-permute-done((bf16[96,1920]{1,0:T(8,128)(2,1)S(1)}, bf16[96,1920]{1,0:T(8,128)(2,1)}, u32[]{:S(2)}, u32[]{:S(2)}) %collective-permute-start.12) | collective-permute-done | bytes 368672 | tf_op jit(solution)/shard_map/ppermute | solution.py:41
  43.3 2.5 %collective-permute-start.16 = (bf16[96,1920]{1,0:T(8,128)(2,1)}, bf16[96,1920]{1,0:T(8,128)(2,1)}, u32[]{:S(2)}, u32[]{:S(2)}) collective-permute-start(bf16[96,1920]{1,0:T(8,128)(2,1)} %collective-permute-done.15.refs_1_), channel_id=1, source_target_pairs={{0,224},{32,0},{64,32},{96,64},{128,96},{160,128},{192,160},{224,1... | collective-permute-start | bytes 1105928 | tf_op jit(solution)/shard_map/ppermute | solution.py:41
  46.7 3.2 %collective-permute-start.28 = (bf16[3072]{0:T(1024)(128)(2,1)S(1)}, bf16[3072]{0:T(1024)(128)(2,1)S(1)}, u32[]{:S(2)}, u32[]{:S(2)}) collective-permute-start(bf16[3072]{0:T(1024)(128)(2,1)S(1)} %dynamic_update_slice.3), channel_id=1, source_target_pairs={{0,224},{32,0},{64,32},{96,64},{128,96},{160,128},{192,160},{224,1... | collective-permute-start | bytes 18440 | tf_op jit(solution)/shard_map/ppermute | solution.py:41
  49.9 18.3 %collective-permute-done.28 = bf16[3072]{0:T(1024)(128)(2,1)S(1)} collective-permute-done((bf16[3072]{0:T(1024)(128)(2,1)S(1)}, bf16[3072]{0:T(1024)(128)(2,1)S(1)}, u32[]{:S(2)}, u32[]{:S(2)}) %collective-permute-start.28) | collective-permute-done | bytes 6176 | tf_op jit(solution)/shard_map/ppermute | solution.py:41
  68.2 3.0 %collective-permute-start.29 = (bf16[3072]{0:T(1024)(128)(2,1)S(1)}, bf16[3072]{0:T(1024)(128)(2,1)S(1)}, u32[]{:S(2)}, u32[]{:S(2)}) collective-permute-start(bf16[3072]{0:T(1024)(128)(2,1)S(1)} %add.44), channel_id=1, source_target_pairs={{0,24},{8,0},{16,8},{24,16},{1,25},{9,1},{17,9},{25,17},{2,26},{10... | collective-permute-start | bytes 18440 | tf_op jit(solution)/shard_map/ppermute | solution.py:41
  74.7 3.0 %collective-permute-done.30 = bf16[3072]{0:T(1024)(128)(2,1)S(1)} collective-permute-done((bf16[3072]{0:T(1024)(128)(2,1)S(1)}, bf16[3072]{0:T(1024)(128)(2,1)S(1)}, u32[]{:S(2)}, u32[]{:S(2)}) %collective-permute-start.30) | collective-permute-done | bytes 6176 | tf_op jit(solution)/shard_map/ppermute | solution.py:41
  80.3 3.4 %collective-permute-done.32 = bf16[3072]{0:T(1024)(128)(2,1)S(1)} collective-permute-done((bf16[3072]{0:T(1024)(128)(2,1)S(1)}, bf16[3072]{0:T(1024)(128)(2,1)S(1)}, u32[]{:S(2)}, u32[]{:S(2)}) %collective-permute-start.32) | collective-permute-done | bytes 6176 | tf_op jit(solution)/shard_map/ppermute | solution.py:41
  83.7 4.9 %collective-permute-start.33 = (bf16[3072]{0:T(1024)(128)(2,1)S(1)}, bf16[3072]{0:T(1024)(128)(2,1)S(1)}, u32[]{:S(2)}, u32[]{:S(2)}) collective-permute-start(bf16[3072]{0:T(1024)(128)(2,1)S(1)} %add.48), channel_id=1, source_target_pairs={{0,192},{32,224},{64,0},{96,32},{128,64},{160,96},{192,128},{224,1... | collective-permute-start | bytes 18440 | tf_op jit(solution)/shard_map/ppermute | solution.py:41
  98.3 2.7 %collective-permute-start.26 = (bf16[192,1920]{1,0:T(8,128)(2,1)S(1)}, bf16[192,1920]{1,0:T(8,128)(2,1)S(1)}, u32[]{:S(2)}, u32[]{:S(2)}) collective-permute-start(bf16[192,1920]{1,0:T(8,128)(2,1)S(1)} %shard_map.142.refs_0_), channel_id=1, source_target_pairs={{0,24},{8,0},{16,8},{24,16},{1,25},{9,1},{17,9},{25,17},{2,26},{10... | collective-permute-start | bytes 2211848 | tf_op jit(solution)/shard_map/ppermute | solution.py:41
  101.0 3.0 %collective-permute-start.4 = (bf16[384,1152]{1,0:T(8,128)(2,1)}, bf16[384,1152]{1,0:T(8,128)(2,1)S(1)}, u32[]{:S(2)}, u32[]{:S(2)}) collective-permute-start(bf16[384,1152]{1,0:T(8,128)(2,1)} %collective-permute-done.3.refs_0_), channel_id=1, source_target_pairs={{0,32},{32,64},{64,96},{96,128},{128,160},{160,192},{192,224},{224... | collective-permute-start | bytes 2654216 | tf_op jit(solution)/shard_map/ppermute | solution.py:41
  104.0 4.3 %collective-permute-done.17.refs_2_ = bf16[96,1920]{1,0:T(8,128)(2,1)S(1)} collective-permute-done((bf16[96,1920]{1,0:T(8,128)(2,1)}, bf16[96,1920]{1,0:T(8,128)(2,1)S(1)}, u32[]{:S(2)}, u32[]{:S(2)}) %collective-permute-start.17) | collective-permute-done | bytes 368672 | tf_op jit(solution)/shard_map/ppermute | solution.py:41
  108.2 3.3 %collective-permute-start.35 = (bf16[3072]{0:T(1024)(128)(2,1)S(1)}, bf16[3072]{0:T(1024)(128)(2,1)S(1)}, u32[]{:S(2)}, u32[]{:S(2)}) collective-permute-start(bf16[3072]{0:T(1024)(128)(2,1)S(1)} %add.50), channel_id=1, source_target_pairs={{0,128},{32,160},{64,192},{96,224},{128,0},{160,32},{192,64},{224,... | collective-permute-start | bytes 18440 | tf_op jit(solution)/shard_map/ppermute | solution.py:41
  112.7 9.4 %collective-permute-done.35 = bf16[3072]{0:T(1024)(128)(2,1)S(1)} collective-permute-done((bf16[3072]{0:T(1024)(128)(2,1)S(1)}, bf16[3072]{0:T(1024)(128)(2,1)S(1)}, u32[]{:S(2)}, u32[]{:S(2)}) %collective-permute-start.35) | collective-permute-done | bytes 6176 | tf_op jit(solution)/shard_map/ppermute | solution.py:41
  125.3 3.0 %collective-permute-start.23 = (bf16[192,1920]{1,0:T(8,128)(2,1)S(1)}, bf16[192,1920]{1,0:T(8,128)(2,1)S(1)}, u32[]{:S(2)}, u32[]{:S(2)}) collective-permute-start(bf16[192,1920]{1,0:T(8,128)(2,1)S(1)} %shard_map.141.refs_0_), channel_id=1, source_target_pairs={{0,24},{8,0},{16,8},{24,16},{1,25},{9,1},{17,9},{25,17},{2,26},{10... | collective-permute-start | bytes 2211848 | tf_op jit(solution)/shard_map/ppermute | solution.py:41
  128.3 6.7 %collective-permute-start.5 = (bf16[384,1152]{1,0:T(8,128)(2,1)S(1)}, bf16[384,1152]{1,0:T(8,128)(2,1)S(1)}, u32[]{:S(2)}, u32[]{:S(2)}) collective-permute-start(bf16[384,1152]{1,0:T(8,128)(2,1)S(1)} %collective-permute-done.4.refs_0_), channel_id=1, source_target_pairs={{0,32},{32,64},{64,96},{96,128},{128,160},{160,192},{192,224},{224... | collective-permute-start | bytes 2654216 | tf_op jit(solution)/shard_map/ppermute | solution.py:41
  135.0 26.1 %collective-permute-done.23.refs_2_ = bf16[192,1920]{1,0:T(8,128)(2,1)S(1)} collective-permute-done((bf16[192,1920]{1,0:T(8,128)(2,1)S(1)}, bf16[192,1920]{1,0:T(8,128)(2,1)S(1)}, u32[]{:S(2)}, u32[]{:S(2)}) %collective-permute-start.23) | collective-permute-done | bytes 737312 | tf_op jit(solution)/shard_map/ppermute | solution.py:41
  161.2 3.2 %collective-permute-start.24 = (bf16[192,1920]{1,0:T(8,128)(2,1)S(1)}, bf16[192,1920]{1,0:T(8,128)(2,1)S(1)}, u32[]{:S(2)}, u32[]{:S(2)}) collective-permute-start(bf16[192,1920]{1,0:T(8,128)(2,1)S(1)} %collective-permute-done.23.refs_2_), channel_id=1, source_target_pairs={{0,24},{8,0},{16,8},{24,16},{1,25},{9,1},{17,9},{25,17},{2,26},{10... | collective-permute-start | bytes 2211848 | tf_op jit(solution)/shard_map/ppermute | solution.py:41
  164.4 2.2 %collective-permute-start.21 = (bf16[176,1920]{1,0:T(8,128)(2,1)S(1)}, bf16[176,1920]{1,0:T(8,128)(2,1)S(1)}, u32[]{:S(2)}, u32[]{:S(2)}) collective-permute-start(bf16[176,1920]{1,0:T(8,128)(2,1)S(1)} %slice.19), channel_id=1, source_target_pairs={{0,24},{8,0},{16,8},{24,16},{1,25},{9,1},{17,9},{25,17},{2,26},{10... | collective-permute-start | bytes 2027528 | tf_op jit(solution)/shard_map/ppermute | solution.py:41
  171.1 3.6 %shard_map.145 = (bf16[1024,3072]{1,0:T(8,128)(2,1)}, bf16[1024,3072]{1,0:T(8,128)(2,1)}, bf16[3072,1024]{1,0:T(8,128)(2,1)}) custom-call(bf16[384,1152]{1,0:T(8,128)(2,1)} %collective-permute-done.3.refs_0_, bf16[384,1152]{1,0:T(8,128)(2,1)} %collective-permute-done.7.refs_1_, ...), custom_call_target="tpu_custom_call", output_to_operand_aliasing={{0}: (2, {}), {1}: (3, {}), {2}: (4, {})} | custom-call | flops 707788800 | bytes 3538944 | tf_op jit(solution)/shard_map/pallas_call | solution.py:201
  174.7 6.9 %collective-permute-done.22.refs_1_ = bf16[192,1920]{1,0:T(8,128)(2,1)S(1)} collective-permute-done((bf16[192,1920]{1,0:T(8,128)(2,1)S(1)}, bf16[192,1920]{1,0:T(8,128)(2,1)S(1)}, u32[]{:S(2)}, u32[]{:S(2)}) %collective-permute-start.22) | collective-permute-done | bytes 737312 | tf_op jit(solution)/shard_map/ppermute | solution.py:41
  181.6 5.2 %collective-permute-start.10 = (bf16[192,1152]{1,0:T(8,128)(2,1)S(1)}, bf16[192,1152]{1,0:T(8,128)(2,1)S(1)}, u32[]{:S(2)}, u32[]{:S(2)}) collective-permute-start(bf16[192,1152]{1,0:T(8,128)(2,1)S(1)} %slice.17), channel_id=1, source_target_pairs={{0,224},{32,0},{64,32},{96,64},{128,96},{160,128},{192,160},{224,1... | collective-permute-start | bytes 1327112 | tf_op jit(solution)/shard_map/ppermute | solution.py:41
  186.8 6.3 %collective-permute-done.27.refs_3_ = bf16[192,1920]{1,0:T(8,128)(2,1)S(1)} collective-permute-done((bf16[192,1920]{1,0:T(8,128)(2,1)S(1)}, bf16[192,1920]{1,0:T(8,128)(2,1)S(1)}, u32[]{:S(2)}, u32[]{:S(2)}) %collective-permute-start.27) | collective-permute-done | bytes 737312 | tf_op jit(solution)/shard_map/ppermute | solution.py:41
  193.1 7.9 %collective-permute-start.6 = (bf16[192,1152]{1,0:T(8,128)(2,1)S(1)}, bf16[192,1152]{1,0:T(8,128)(2,1)S(1)}, u32[]{:S(2)}, u32[]{:S(2)}) collective-permute-start(bf16[192,1152]{1,0:T(8,128)(2,1)S(1)} %slice.16), channel_id=1, source_target_pairs={{0,32},{32,64},{64,96},{96,128},{128,160},{160,192},{192,224},{224... | collective-permute-start | bytes 1327112 | tf_op jit(solution)/shard_map/ppermute | solution.py:41
  201.0 3.5 %shard_map.146 = (bf16[1024,3072]{1,0:T(8,128)(2,1)}, bf16[1024,3072]{1,0:T(8,128)(2,1)}, bf16[3072,1024]{1,0:T(8,128)(2,1)}) custom-call(bf16[192,1920]{1,0:T(8,128)(2,1)S(1)} %shard_map.142.refs_0_, bf16[192,1920]{1,0:T(8,128)(2,1)S(1)} %collective-permute-done.25.refs_1_, ...), custom_call_target="tpu_custom_call", output_to_operand_aliasing={{0}: (4, {}), {1}: (5, {}), {2}: (6, {})} | custom-call | flops 1179648000 | bytes 5898240 | tf_op jit(solution)/shard_map/pallas_call | solution.py:201
  204.4 3.5 %shard_map.147 = (bf16[1024,3072]{1,0:T(8,128)(2,1)}, bf16[1024,3072]{1,0:T(8,128)(2,1)}, bf16[3072,1024]{1,0:T(8,128)(2,1)}) custom-call(bf16[192,1920]{1,0:T(8,128)(2,1)S(1)} %shard_map.141.refs_0_, bf16[192,1920]{1,0:T(8,128)(2,1)S(1)} %collective-permute-done.22.refs_1_, ...), custom_call_target="tpu_custom_call", output_to_operand_aliasing={{0}: (4, {}), {1}: (5, {}), {2}: (6, {})} | custom-call | flops 1179648000 | bytes 5898240 | tf_op jit(solution)/shard_map/pallas_call | solution.py:201
  207.9 2.8 %shard_map.148 = (bf16[1024,3072]{1,0:T(8,128)(2,1)}, bf16[1024,3072]{1,0:T(8,128)(2,1)}, bf16[3072,1024]{1,0:T(8,128)(2,1)}) custom-call(bf16[384,1152]{1,0:T(8,128)(2,1)S(1)} %collective-permute-done.4.refs_0_, bf16[384,1152]{1,0:T(8,128)(2,1)S(1)} %collective-permute-done.8.refs_1_, ...), custom_call_target="tpu_custom_call", output_to_operand_aliasing={{0}: (2, {}), {1}: (3, {}), {2}: (4, {})} | custom-call | flops 707788800 | bytes 3538944 | tf_op jit(solution)/shard_map/pallas_call | solution.py:201
  210.7 2.8 %shard_map.149 = (bf16[1024,3072]{1,0:T(8,128)(2,1)}, bf16[1024,3072]{1,0:T(8,128)(2,1)}, bf16[3072,1024]{1,0:T(8,128)(2,1)}) custom-call(bf16[384,1152]{1,0:T(8,128)(2,1)S(1)} %collective-permute-done.5.refs_0_, bf16[384,1152]{1,0:T(8,128)(2,1)S(1)} %collective-permute-done.9.refs_1_, ...), custom_call_target="tpu_custom_call", output_to_operand_aliasing={{0}: (2, {}), {1}: (3, {}), {2}: (4, {})} | custom-call | flops 707788800 | bytes 3538944 | tf_op jit(solution)/shard_map/pallas_call | solution.py:201
  213.5 4.8 %shard_map.150 = (bf16[1024,3072]{1,0:T(8,128)(2,1)}, bf16[1024,3072]{1,0:T(8,128)(2,1)}, bf16[3072,1024]{1,0:T(8,128)(2,1)}) custom-call(bf16[288,1920]{1,0:T(8,128)(2,1)S(1)} %shard_map.140.refs_0_, bf16[288,1920]{1,0:T(8,128)(2,1)S(1)} %collective-permute-done.18.refs_1_, ...), custom_call_target="tpu_custom_call", output_to_operand_aliasing={{0}: (5, {}), {1}: (6, {}), {2}: (7, {})} | custom-call | flops 1769472000 | bytes 8847360 | tf_op jit(solution)/shard_map/pallas_call | solution.py:201
  (81 shorter events, 40.2 us)
Async XLA Ops:
  3.1 16.6 %collective-permute-start = (bf16[96,3072]{1,0:T(8,128)(2,1)}, bf16[96,3072]{1,0:T(8,128)(2,1)S(1)}, u32[]{:S(2)}, u32[]{:S(2)}) collective-permute-start(bf16[96,3072]{1,0:T(8,128)(2,1)} %get-tuple-element.33.refs_0_), channel_id=1, source_target_pairs={{0,8},{8,16},{16,24},{24,0},{1,9},{9,17},{17,25},{25,1},{2,10},{10... | collective-permute-start | bytes 1769480 | tf_op jit(solution)/shard_map/ppermute | solution.py:41
  4.8 29.1 %collective-permute-start.1 = (bf16[96,3072]{1,0:T(8,128)(2,1)}, bf16[96,3072]{1,0:T(8,128)(2,1)S(1)}, u32[]{:S(2)}, u32[]{:S(2)}) collective-permute-start(bf16[96,3072]{1,0:T(8,128)(2,1)} %get-tuple-element.33.refs_0_), channel_id=1, source_target_pairs={{0,24},{8,0},{16,8},{24,16},{1,25},{9,1},{17,9},{25,17},{2,26},{10... | collective-permute-start | bytes 1769480 | tf_op jit(solution)/shard_map/ppermute | solution.py:41
  19.8 15.5 %collective-permute-start.2 = (bf16[96,3072]{1,0:T(8,128)(2,1)S(1)}, bf16[96,3072]{1,0:T(8,128)(2,1)S(1)}, u32[]{:S(2)}, u32[]{:S(2)}) collective-permute-start(bf16[96,3072]{1,0:T(8,128)(2,1)S(1)} %collective-permute-done.refs_1_), channel_id=1, source_target_pairs={{0,8},{8,16},{16,24},{24,0},{1,9},{9,17},{17,25},{25,1},{2,10},{10... | collective-permute-start | bytes 1769480 | tf_op jit(solution)/shard_map/ppermute | solution.py:41
  20.1 9.5 %collective-permute-start.11 = (bf16[96,1920]{1,0:T(8,128)(2,1)}, bf16[96,1920]{1,0:T(8,128)(2,1)S(1)}, u32[]{:S(2)}, u32[]{:S(2)}) collective-permute-start(bf16[96,1920]{1,0:T(8,128)(2,1)} %get-tuple-element.34), channel_id=1, source_target_pairs={{0,32},{32,64},{64,96},{96,128},{128,160},{160,192},{192,224},{224... | collective-permute-start | bytes 1105928 | tf_op jit(solution)/shard_map/ppermute | solution.py:41
  22.0 9.4 %collective-permute-start.14 = (bf16[96,1920]{1,0:T(8,128)(2,1)}, bf16[96,1920]{1,0:T(8,128)(2,1)S(1)}, u32[]{:S(2)}, u32[]{:S(2)}) collective-permute-start(bf16[96,1920]{1,0:T(8,128)(2,1)} %get-tuple-element.34), channel_id=1, source_target_pairs={{0,224},{32,0},{64,32},{96,64},{128,96},{160,128},{192,160},{224,1... | collective-permute-start | bytes 1105928 | tf_op jit(solution)/shard_map/ppermute | solution.py:41
  29.5 13.8 %collective-permute-start.12 = (bf16[96,1920]{1,0:T(8,128)(2,1)S(1)}, bf16[96,1920]{1,0:T(8,128)(2,1)}, u32[]{:S(2)}, u32[]{:S(2)}) collective-permute-start(bf16[96,1920]{1,0:T(8,128)(2,1)S(1)} %collective-permute-done.11.refs_0_), channel_id=1, source_target_pairs={{0,32},{32,64},{64,96},{96,128},{128,160},{160,192},{192,224},{224... | collective-permute-start | bytes 1105928 | tf_op jit(solution)/shard_map/ppermute | solution.py:41
  31.4 11.9 %collective-permute-start.15 = (bf16[96,1920]{1,0:T(8,128)(2,1)S(1)}, bf16[96,1920]{1,0:T(8,128)(2,1)}, u32[]{:S(2)}, u32[]{:S(2)}) collective-permute-start(bf16[96,1920]{1,0:T(8,128)(2,1)S(1)} %collective-permute-done.14.refs_1_), channel_id=1, source_target_pairs={{0,224},{32,0},{64,32},{96,64},{128,96},{160,128},{192,160},{224,1... | collective-permute-start | bytes 1105928 | tf_op jit(solution)/shard_map/ppermute | solution.py:41
  36.5 64.5 %collective-permute-start.3 = (bf16[384,1152]{1,0:T(8,128)(2,1)S(1)}, bf16[384,1152]{1,0:T(8,128)(2,1)}, u32[]{:S(2)}, u32[]{:S(2)}) collective-permute-start(bf16[384,1152]{1,0:T(8,128)(2,1)S(1)} %shard_map.139.refs_0_), channel_id=1, source_target_pairs={{0,32},{32,64},{64,96},{96,128},{128,160},{160,192},{192,224},{224... | collective-permute-start | bytes 2654216 | tf_op jit(solution)/shard_map/ppermute | solution.py:41
  38.5 65.4 %collective-permute-start.7 = (bf16[384,1152]{1,0:T(8,128)(2,1)S(1)}, bf16[384,1152]{1,0:T(8,128)(2,1)}, u32[]{:S(2)}, u32[]{:S(2)}) collective-permute-start(bf16[384,1152]{1,0:T(8,128)(2,1)S(1)} %shard_map.139.refs_0_), channel_id=1, source_target_pairs={{0,224},{32,0},{64,32},{96,64},{128,96},{160,128},{192,160},{224,1... | collective-permute-start | bytes 2654216 | tf_op jit(solution)/shard_map/ppermute | solution.py:41
  43.3 53.3 %collective-permute-start.13 = (bf16[96,1920]{1,0:T(8,128)(2,1)}, bf16[96,1920]{1,0:T(8,128)(2,1)}, u32[]{:S(2)}, u32[]{:S(2)}) collective-permute-start(bf16[96,1920]{1,0:T(8,128)(2,1)} %collective-permute-done.12.refs_0_), channel_id=1, source_target_pairs={{0,32},{32,64},{64,96},{96,128},{128,160},{160,192},{192,224},{224... | collective-permute-start | bytes 1105928 | tf_op jit(solution)/shard_map/ppermute | solution.py:41
  43.3 55.0 %collective-permute-start.16 = (bf16[96,1920]{1,0:T(8,128)(2,1)}, bf16[96,1920]{1,0:T(8,128)(2,1)}, u32[]{:S(2)}, u32[]{:S(2)}) collective-permute-start(bf16[96,1920]{1,0:T(8,128)(2,1)} %collective-permute-done.15.refs_1_), channel_id=1, source_target_pairs={{0,224},{32,0},{64,32},{96,64},{128,96},{160,128},{192,160},{224,1... | collective-permute-start | bytes 1105928 | tf_op jit(solution)/shard_map/ppermute | solution.py:41
  46.7 21.4 %collective-permute-start.28 = (bf16[3072]{0:T(1024)(128)(2,1)S(1)}, bf16[3072]{0:T(1024)(128)(2,1)S(1)}, u32[]{:S(2)}, u32[]{:S(2)}) collective-permute-start(bf16[3072]{0:T(1024)(128)(2,1)S(1)} %dynamic_update_slice.3), channel_id=1, source_target_pairs={{0,224},{32,0},{64,32},{96,64},{128,96},{160,128},{192,160},{224,1... | collective-permute-start | bytes 18440 | tf_op jit(solution)/shard_map/ppermute | solution.py:41
  72.5 5.1 %collective-permute-start.30 = (bf16[3072]{0:T(1024)(128)(2,1)S(1)}, bf16[3072]{0:T(1024)(128)(2,1)S(1)}, u32[]{:S(2)}, u32[]{:S(2)}) collective-permute-start(bf16[3072]{0:T(1024)(128)(2,1)S(1)} %add.45), channel_id=1, source_target_pairs={{0,16},{8,24},{16,0},{24,8},{1,17},{9,25},{17,1},{25,9},{2,18},{10... | collective-permute-start | bytes 18440 | tf_op jit(solution)/shard_map/ppermute | solution.py:41
  83.7 6.9 %collective-permute-start.33 = (bf16[3072]{0:T(1024)(128)(2,1)S(1)}, bf16[3072]{0:T(1024)(128)(2,1)S(1)}, u32[]{:S(2)}, u32[]{:S(2)}) collective-permute-start(bf16[3072]{0:T(1024)(128)(2,1)S(1)} %add.48), channel_id=1, source_target_pairs={{0,192},{32,224},{64,0},{96,32},{128,64},{160,96},{192,128},{224,1... | collective-permute-start | bytes 18440 | tf_op jit(solution)/shard_map/ppermute | solution.py:41
  95.7 28.1 %collective-permute-start.25 = (bf16[192,1920]{1,0:T(8,128)(2,1)S(1)}, bf16[192,1920]{1,0:T(8,128)(2,1)S(1)}, u32[]{:S(2)}, u32[]{:S(2)}) collective-permute-start(bf16[192,1920]{1,0:T(8,128)(2,1)S(1)} %shard_map.142.refs_0_), channel_id=1, source_target_pairs={{0,8},{8,16},{16,24},{24,0},{1,9},{9,17},{17,25},{25,1},{2,10},{10... | collective-permute-start | bytes 2211848 | tf_op jit(solution)/shard_map/ppermute | solution.py:41
  96.6 11.7 %collective-permute-start.17 = (bf16[96,1920]{1,0:T(8,128)(2,1)}, bf16[96,1920]{1,0:T(8,128)(2,1)S(1)}, u32[]{:S(2)}, u32[]{:S(2)}) collective-permute-start(bf16[96,1920]{1,0:T(8,128)(2,1)} %collective-permute-done.13.refs_0_), channel_id=1, source_target_pairs={{0,32},{32,64},{64,96},{96,128},{128,160},{160,192},{192,224},{224... | collective-permute-start | bytes 1105928 | tf_op jit(solution)/shard_map/ppermute | solution.py:41
  98.3 27.0 %collective-permute-start.26 = (bf16[192,1920]{1,0:T(8,128)(2,1)S(1)}, bf16[192,1920]{1,0:T(8,128)(2,1)S(1)}, u32[]{:S(2)}, u32[]{:S(2)}) collective-permute-start(bf16[192,1920]{1,0:T(8,128)(2,1)S(1)} %shard_map.142.refs_0_), channel_id=1, source_target_pairs={{0,24},{8,0},{16,8},{24,16},{1,25},{9,1},{17,9},{25,17},{2,26},{10... | collective-permute-start | bytes 2211848 | tf_op jit(solution)/shard_map/ppermute | solution.py:41
  101.0 27.3 %collective-permute-start.4 = (bf16[384,1152]{1,0:T(8,128)(2,1)}, bf16[384,1152]{1,0:T(8,128)(2,1)S(1)}, u32[]{:S(2)}, u32[]{:S(2)}) collective-permute-start(bf16[384,1152]{1,0:T(8,128)(2,1)} %collective-permute-done.3.refs_0_), channel_id=1, source_target_pairs={{0,32},{32,64},{64,96},{96,128},{128,160},{160,192},{192,224},{224... | collective-permute-start | bytes 2654216 | tf_op jit(solution)/shard_map/ppermute | solution.py:41
  103.9 31.0 %collective-permute-start.8 = (bf16[384,1152]{1,0:T(8,128)(2,1)}, bf16[384,1152]{1,0:T(8,128)(2,1)S(1)}, u32[]{:S(2)}, u32[]{:S(2)}) collective-permute-start(bf16[384,1152]{1,0:T(8,128)(2,1)} %collective-permute-done.7.refs_1_), channel_id=1, source_target_pairs={{0,224},{32,0},{64,32},{96,64},{128,96},{160,128},{192,160},{224,1... | collective-permute-start | bytes 2654216 | tf_op jit(solution)/shard_map/ppermute | solution.py:41
  108.2 13.9 %collective-permute-start.35 = (bf16[3072]{0:T(1024)(128)(2,1)S(1)}, bf16[3072]{0:T(1024)(128)(2,1)S(1)}, u32[]{:S(2)}, u32[]{:S(2)}) collective-permute-start(bf16[3072]{0:T(1024)(128)(2,1)S(1)} %add.50), channel_id=1, source_target_pairs={{0,128},{32,160},{64,192},{96,224},{128,0},{160,32},{192,64},{224,... | collective-permute-start | bytes 18440 | tf_op jit(solution)/shard_map/ppermute | solution.py:41
  122.1 38.9 %collective-permute-start.19 = (bf16[288,1920]{1,0:T(8,128)(2,1)S(1)}, bf16[288,1920]{1,0:T(8,128)(2,1)S(1)}, u32[]{:S(2)}, u32[]{:S(2)}) collective-permute-start(bf16[288,1920]{1,0:T(8,128)(2,1)S(1)} %shard_map.140.refs_0_), channel_id=1, source_target_pairs={{0,24},{8,0},{16,8},{24,16},{1,25},{9,1},{17,9},{25,17},{2,26},{10... | collective-permute-start | bytes 3317768 | tf_op jit(solution)/shard_map/ppermute | solution.py:41
  123.8 37.4 %collective-permute-start.18 = (bf16[288,1920]{1,0:T(8,128)(2,1)S(1)}, bf16[288,1920]{1,0:T(8,128)(2,1)S(1)}, u32[]{:S(2)}, u32[]{:S(2)}) collective-permute-start(bf16[288,1920]{1,0:T(8,128)(2,1)S(1)} %shard_map.140.refs_0_), channel_id=1, source_target_pairs={{0,8},{8,16},{16,24},{24,0},{1,9},{9,17},{17,25},{25,1},{2,10},{10... | collective-permute-start | bytes 3317768 | tf_op jit(solution)/shard_map/ppermute | solution.py:41
  125.3 35.8 %collective-permute-start.23 = (bf16[192,1920]{1,0:T(8,128)(2,1)S(1)}, bf16[192,1920]{1,0:T(8,128)(2,1)S(1)}, u32[]{:S(2)}, u32[]{:S(2)}) collective-permute-start(bf16[192,1920]{1,0:T(8,128)(2,1)S(1)} %shard_map.141.refs_0_), channel_id=1, source_target_pairs={{0,24},{8,0},{16,8},{24,16},{1,25},{9,1},{17,9},{25,17},{2,26},{10... | collective-permute-start | bytes 2211848 | tf_op jit(solution)/shard_map/ppermute | solution.py:41
  128.3 36.2 %collective-permute-start.5 = (bf16[384,1152]{1,0:T(8,128)(2,1)S(1)}, bf16[384,1152]{1,0:T(8,128)(2,1)S(1)}, u32[]{:S(2)}, u32[]{:S(2)}) collective-permute-start(bf16[384,1152]{1,0:T(8,128)(2,1)S(1)} %collective-permute-done.4.refs_0_), channel_id=1, source_target_pairs={{0,32},{32,64},{64,96},{96,128},{128,160},{160,192},{192,224},{224... | collective-permute-start | bytes 2654216 | tf_op jit(solution)/shard_map/ppermute | solution.py:41
  135.0 34.2 %collective-permute-start.9 = (bf16[384,1152]{1,0:T(8,128)(2,1)S(1)}, bf16[384,1152]{1,0:T(8,128)(2,1)S(1)}, u32[]{:S(2)}, u32[]{:S(2)}) collective-permute-start(bf16[384,1152]{1,0:T(8,128)(2,1)S(1)} %collective-permute-done.8.refs_1_), channel_id=1, source_target_pairs={{0,224},{32,0},{64,32},{96,64},{128,96},{160,128},{192,160},{224,1... | collective-permute-start | bytes 2654216 | tf_op jit(solution)/shard_map/ppermute | solution.py:41
  161.0 20.6 %collective-permute-start.22 = (bf16[192,1920]{1,0:T(8,128)(2,1)S(1)}, bf16[192,1920]{1,0:T(8,128)(2,1)S(1)}, u32[]{:S(2)}, u32[]{:S(2)}) collective-permute-start(bf16[192,1920]{1,0:T(8,128)(2,1)S(1)} %shard_map.141.refs_0_), channel_id=1, source_target_pairs={{0,8},{8,16},{16,24},{24,0},{1,9},{9,17},{17,25},{25,1},{2,10},{10... | collective-permute-start | bytes 2211848 | tf_op jit(solution)/shard_map/ppermute | solution.py:41
  161.1 32.1 %collective-permute-start.27 = (bf16[192,1920]{1,0:T(8,128)(2,1)S(1)}, bf16[192,1920]{1,0:T(8,128)(2,1)S(1)}, u32[]{:S(2)}, u32[]{:S(2)}) collective-permute-start(bf16[192,1920]{1,0:T(8,128)(2,1)S(1)} %collective-permute-done.25.refs_1_), channel_id=1, source_target_pairs={{0,8},{8,16},{16,24},{24,0},{1,9},{9,17},{17,25},{25,1},{2,10},{10... | collective-permute-start | bytes 2211848 | tf_op jit(solution)/shard_map/ppermute | solution.py:41
  161.2 43.2 %collective-permute-start.24 = (bf16[192,1920]{1,0:T(8,128)(2,1)S(1)}, bf16[192,1920]{1,0:T(8,128)(2,1)S(1)}, u32[]{:S(2)}, u32[]{:S(2)}) collective-permute-start(bf16[192,1920]{1,0:T(8,128)(2,1)S(1)} %collective-permute-done.23.refs_2_), channel_id=1, source_target_pairs={{0,24},{8,0},{16,8},{24,16},{1,25},{9,1},{17,9},{25,17},{2,26},{10... | collective-permute-start | bytes 2211848 | tf_op jit(solution)/shard_map/ppermute | solution.py:41
  164.4 49.1 %collective-permute-start.21 = (bf16[176,1920]{1,0:T(8,128)(2,1)S(1)}, bf16[176,1920]{1,0:T(8,128)(2,1)S(1)}, u32[]{:S(2)}, u32[]{:S(2)}) collective-permute-start(bf16[176,1920]{1,0:T(8,128)(2,1)S(1)} %slice.19), channel_id=1, source_target_pairs={{0,24},{8,0},{16,8},{24,16},{1,25},{9,1},{17,9},{25,17},{2,26},{10... | collective-permute-start | bytes 2027528 | tf_op jit(solution)/shard_map/ppermute | solution.py:41
  169.1 44.4 %collective-permute-start.20 = (bf16[112,1920]{1,0:T(8,128)(2,1)S(1)}, bf16[112,1920]{1,0:T(8,128)(2,1)S(1)}, u32[]{:S(2)}, u32[]{:S(2)}) collective-permute-start(bf16[112,1920]{1,0:T(8,128)(2,1)S(1)} %slice.18), channel_id=1, source_target_pairs={{0,8},{8,16},{16,24},{24,0},{1,9},{9,17},{17,25},{25,1},{2,10},{10... | collective-permute-start | bytes 1290248 | tf_op jit(solution)/shard_map/ppermute | solution.py:41
  181.6 36.7 %collective-permute-start.10 = (bf16[192,1152]{1,0:T(8,128)(2,1)S(1)}, bf16[192,1152]{1,0:T(8,128)(2,1)S(1)}, u32[]{:S(2)}, u32[]{:S(2)}) collective-permute-start(bf16[192,1152]{1,0:T(8,128)(2,1)S(1)} %slice.17), channel_id=1, source_target_pairs={{0,224},{32,0},{64,32},{96,64},{128,96},{160,128},{192,160},{224,1... | collective-permute-start | bytes 1327112 | tf_op jit(solution)/shard_map/ppermute | solution.py:41
  193.1 25.2 %collective-permute-start.6 = (bf16[192,1152]{1,0:T(8,128)(2,1)S(1)}, bf16[192,1152]{1,0:T(8,128)(2,1)S(1)}, u32[]{:S(2)}, u32[]{:S(2)}) collective-permute-start(bf16[192,1152]{1,0:T(8,128)(2,1)S(1)} %slice.16), channel_id=1, source_target_pairs={{0,32},{32,64},{64,96},{96,128},{128,160},{160,192},{192,224},{224... | collective-permute-start | bytes 1327112 | tf_op jit(solution)/shard_map/ppermute | solution.py:41
  (10 other events, 170.3 us)

commit v2 on v1

--- a/solution.py
+++ b/solution.py
@@ -25,7 +25,7 @@
 A_COLS = WIDE + CUT
 B_COLS = WIDE + WIDE - CUT
 STEP = 128
-UP = 192
+UP = 160
 GRANT = 1 << 20
 
 ANY = pl.BlockSpec(memory_space=pl.ANY)
@@ -164,13 +164,17 @@
         for start, width, out, row, k in groups:
             base = start if kind == "a" else start - WIDE
 
-            def turn(i, _, start=start, base=base, b=b):
-                src = pl.multiple_of(start + i * STEP, STEP)
-                dst = pl.multiple_of(base + i * STEP, STEP)
-                turned[b, pl.ds(dst, STEP), :] = held[b, :, pl.ds(src, STEP)].T
+            def turn(i, _, start=start, base=base, b=b, step=4 * STEP):
+                src = pl.multiple_of(start + i * step, STEP)
+                dst = pl.multiple_of(base + i * step, STEP)
+                turned[b, pl.ds(dst, step), :] = held[b, :, pl.ds(src, step)].T
                 return 0
 
-            lax.fori_loop(0, width // STEP, turn, 0)
+            whole, rest = divmod(width, 4 * STEP)
+            lax.fori_loop(0, whole, turn, 0)
+            if rest:
+                last = width - rest
+                turn(0, 0, start + last, base + last, b, rest)
             c = pltpu.make_async_copy(
                 turned.at[b, pl.ds(base, width)],
                 out.at[pl.ds(row, width), cols],
@@ -331,13 +335,13 @@
     full = added(full, n5)
     n6 = sent(6, full)
     outs = placed(outs, b_blocks((6, 2), 0), (s2, l2, r2, o2))
-    outs = placed(outs, (a_block(6, 0), a_block(2, 1)), (p2, q2))
+    full = added(full, n6)
+    n7 = sent(7, full)
     b3 = shifted(r3[part:], y, -1)
     t3 = shifted(l3[:part], y, 1)
     q4 = shifted(q3[UP:], z, -1)
     p4 = shifted(p3[:UP], z, 1)
-    full = added(full, n6)
-    n7 = sent(7, full)
+    outs = placed(outs, (a_block(6, 0), a_block(2, 1)), (p2, q2))
     outs = placed(outs, (a_block(5, 0), a_block(3, 1)), (p3, q3))
     near = [[(s, i * ROWS, ROWS, r, 0) for s, r in enumerate((0, 3, 1))] for i in range(3)]
     cut = part - ROWS
@@ -346,6 +350,7 @@
         ((3, ROWS, cut, 2, 0), (4, 0, ROWS - cut, 2, cut)),
         ((4, ROWS - cut, ROWS, 2, 0),),
     )
+    full = added(full, n7)
     outs = placed(
         outs,
         tuple(
@@ -356,7 +361,6 @@
     outs = placed(
         outs, (("a", 4, ((0, 0, UP, None, 0), (1, 0, BLOCK - UP, None, UP))),), (p4, q4)
     )
-    full = added(full, n7)
     return (*outs, full)
 
 

time: 221 us -> 193 us (0.87)
  the two profiles are of different devices: /device:TPU:32 before, /device:TPU:6 now
where the time goes in v2:
time: 193 us; the launch traced here: 192 us
  waiting for transfers between devices  98.6 us (51%)
  starting transfers between devices  60.4 us (31%)
  Pallas kernels  26.8 us (14%)
  local copies, waits for them, and re-layouts  4.15 us (2%)
    ppermute x36, waiting for transfers between devices, shifted(): return lax.ppermute(x, axis, [(i, (i + step) % n) for i in range(n)])  98.6 us
    ppermute x36, starting transfers between devices, shifted(): return lax.ppermute(x, axis, [(i, (i + step) % n) for i in range(n)])  60.4 us
    pallas_call x9, Pallas kernels, placed(): pl.pallas_call(functools.partial(place_body, first, blocks, len(srcs)), o...  21.6 us
  transfers between devices with their start and end apart: 36, of which 16 were waited for; matrix products, arithmetic and copies ran while one was open for 1% of the time, Pallas kernels for 12%

profile of v2, /device:TPU:6, one launch (start us, length us, event | category | flops | bytes accessed | tf_op | source)
XLA Modules:
  0.0 192.4 jit_solution(7275386907215983888)
XLA Ops:
  0.6 2.5 %shard_map.138 = (bf16[96,3072]{1,0:T(8,128)(2,1)}, bf16[96,1920]{1,0:T(8,128)(2,1)}) custom-call(bf16[96,1024]{1,0:T(8,128)(2,1)} %refs_0_.1, bf16[16,96]{1,0:T(8,128)(2,1)} %bitcast.6, bf16[16,1024]{1,0:T(8,128)(2,1)} %refs_2_.1, bf16[96,1024]{1,0:T(8,128)(2,1)} %bitcast.4, bf16[16,96]{1,0:T(8,128)(2,1)} %refs_4_.1, bf16[16,1024]{1,0:T(8,128)(2,1)} %bitcast.5, ...), custom_call_target="tpu_custom_call" | custom-call | tf_op jit(solution)/shard_map/pallas_call | solution.py:73
  4.8 1.9 collective-permute-start.11
  6.7 3.9 %collective-permute-start.14 = (bf16[96,1920]{1,0:T(8,128)(2,1)}, bf16[96,1920]{1,0:T(8,128)(2,1)S(1)}, u32[]{:S(2)}, u32[]{:S(2)}) collective-permute-start(bf16[96,1920]{1,0:T(8,128)(2,1)} %get-tuple-element.34), channel_id=1, source_target_pairs={{0,224},{32,0},{64,32},{96,64},{128,96},{160,128},{192,160},{224,1... | collective-permute-start | bytes 1105928 | tf_op jit(solution)/shard_map/ppermute | solution.py:41
  12.3 7.5 %collective-permute-done.refs_1_ = bf16[96,3072]{1,0:T(8,128)(2,1)S(1)} collective-permute-done((bf16[96,3072]{1,0:T(8,128)(2,1)}, bf16[96,3072]{1,0:T(8,128)(2,1)S(1)}, u32[]{:S(2)}, u32[]{:S(2)}) %collective-permute-start) | collective-permute-done | bytes 589856 | tf_op jit(solution)/shard_map/ppermute | solution.py:41
  20.1 1.9 collective-permute-start.12
  22.7 3.9 %collective-permute-start.15 = (bf16[96,1920]{1,0:T(8,128)(2,1)S(1)}, bf16[96,1920]{1,0:T(8,128)(2,1)}, u32[]{:S(2)}, u32[]{:S(2)}) collective-permute-start(bf16[96,1920]{1,0:T(8,128)(2,1)S(1)} %collective-permute-done.14.refs_1_), channel_id=1, source_target_pairs={{0,224},{32,0},{64,32},{96,64},{128,96},{160,128},{192,160},{224,1... | collective-permute-start | bytes 1105928 | tf_op jit(solution)/shard_map/ppermute | solution.py:41
  26.7 6.9 %collective-permute-done.12.refs_0_ = bf16[96,1920]{1,0:T(8,128)(2,1)} collective-permute-done((bf16[96,1920]{1,0:T(8,128)(2,1)S(1)}, bf16[96,1920]{1,0:T(8,128)(2,1)}, u32[]{:S(2)}, u32[]{:S(2)}) %collective-permute-start.12) | collective-permute-done | bytes 368672 | tf_op jit(solution)/shard_map/ppermute | solution.py:41
  36.5 6.0 %collective-permute-start.7 = (bf16[384,1152]{1,0:T(8,128)(2,1)S(1)}, bf16[384,1152]{1,0:T(8,128)(2,1)}, u32[]{:S(2)}, u32[]{:S(2)}) collective-permute-start(bf16[384,1152]{1,0:T(8,128)(2,1)S(1)} %shard_map.139.refs_0_), channel_id=1, source_target_pairs={{0,224},{32,0},{64,32},{96,64},{128,96},{160,128},{192,160},{224,1... | collective-permute-start | bytes 2654216 | tf_op jit(solution)/shard_map/ppermute | solution.py:41
  45.4 2.2 %collective-permute-start.28 = (bf16[3072]{0:T(1024)(128)(2,1)S(1)}, bf16[3072]{0:T(1024)(128)(2,1)S(1)}, u32[]{:S(2)}, u32[]{:S(2)}) collective-permute-start(bf16[3072]{0:T(1024)(128)(2,1)S(1)} %dynamic_update_slice.3), channel_id=1, source_target_pairs={{0,224},{32,0},{64,32},{96,64},{128,96},{160,128},{192,160},{224,1... | collective-permute-start | bytes 18440 | tf_op jit(solution)/shard_map/ppermute | solution.py:41
  47.6 20.2 %collective-permute-done.28 = bf16[3072]{0:T(1024)(128)(2,1)S(1)} collective-permute-done((bf16[3072]{0:T(1024)(128)(2,1)S(1)}, bf16[3072]{0:T(1024)(128)(2,1)S(1)}, u32[]{:S(2)}, u32[]{:S(2)}) %collective-permute-start.28) | collective-permute-done | bytes 6176 | tf_op jit(solution)/shard_map/ppermute | solution.py:41
  68.3 3.1 %collective-permute-done.29 = bf16[3072]{0:T(1024)(128)(2,1)S(1)} collective-permute-done((bf16[3072]{0:T(1024)(128)(2,1)S(1)}, bf16[3072]{0:T(1024)(128)(2,1)S(1)}, u32[]{:S(2)}, u32[]{:S(2)}) %collective-permute-start.29) | collective-permute-done | bytes 6176 | tf_op jit(solution)/shard_map/ppermute | solution.py:41
  72.1 4.5 %collective-permute-done.30 = bf16[3072]{0:T(1024)(128)(2,1)S(1)} collective-permute-done((bf16[3072]{0:T(1024)(128)(2,1)S(1)}, bf16[3072]{0:T(1024)(128)(2,1)S(1)}, u32[]{:S(2)}, u32[]{:S(2)}) %collective-permute-start.30) | collective-permute-done | bytes 6176 | tf_op jit(solution)/shard_map/ppermute | solution.py:41
  78.2 3.2 %collective-permute-done.32 = bf16[3072]{0:T(1024)(128)(2,1)S(1)} collective-permute-done((bf16[3072]{0:T(1024)(128)(2,1)S(1)}, bf16[3072]{0:T(1024)(128)(2,1)S(1)}, u32[]{:S(2)}, u32[]{:S(2)}) %collective-permute-start.32) | collective-permute-done | bytes 6176 | tf_op jit(solution)/shard_map/ppermute | solution.py:41
  81.4 2.9 %collective-permute-start.33 = (bf16[3072]{0:T(1024)(128)(2,1)S(1)}, bf16[3072]{0:T(1024)(128)(2,1)S(1)}, u32[]{:S(2)}, u32[]{:S(2)}) collective-permute-start(bf16[3072]{0:T(1024)(128)(2,1)S(1)} %add.48), channel_id=1, source_target_pairs={{0,192},{32,224},{64,0},{96,32},{128,64},{160,96},{192,128},{224,1... | collective-permute-start | bytes 18440 | tf_op jit(solution)/shard_map/ppermute | solution.py:41
  87.3 3.7 %collective-permute-done.34 = bf16[3072]{0:T(1024)(128)(2,1)S(1)} collective-permute-done((bf16[3072]{0:T(1024)(128)(2,1)S(1)}, bf16[3072]{0:T(1024)(128)(2,1)S(1)}, u32[]{:S(2)}, u32[]{:S(2)}) %collective-permute-start.34) | collective-permute-done | bytes 6176 | tf_op jit(solution)/shard_map/ppermute | solution.py:41
  91.1 3.8 %collective-permute-start.35 = (bf16[3072]{0:T(1024)(128)(2,1)S(1)}, bf16[3072]{0:T(1024)(128)(2,1)S(1)}, u32[]{:S(2)}, u32[]{:S(2)}) collective-permute-start(bf16[3072]{0:T(1024)(128)(2,1)S(1)} %add.50), channel_id=1, source_target_pairs={{0,128},{32,160},{64,192},{96,224},{128,0},{160,32},{192,64},{224,... | collective-permute-start | bytes 18440 | tf_op jit(solution)/shard_map/ppermute | solution.py:41
  98.7 3.2 %collective-permute-start.26 = (bf16[192,1920]{1,0:T(8,128)(2,1)S(1)}, bf16[192,1920]{1,0:T(8,128)(2,1)S(1)}, u32[]{:S(2)}, u32[]{:S(2)}) collective-permute-start(bf16[192,1920]{1,0:T(8,128)(2,1)S(1)} %shard_map.142.refs_0_), channel_id=1, source_target_pairs={{0,24},{8,0},{16,8},{24,16},{1,25},{9,1},{17,9},{25,17},{2,26},{10... | collective-permute-start | bytes 2211848 | tf_op jit(solution)/shard_map/ppermute | solution.py:41
  105.5 2.9 %collective-permute-start.8 = (bf16[384,1152]{1,0:T(8,128)(2,1)}, bf16[384,1152]{1,0:T(8,128)(2,1)S(1)}, u32[]{:S(2)}, u32[]{:S(2)}) collective-permute-start(bf16[384,1152]{1,0:T(8,128)(2,1)} %collective-permute-done.7.refs_1_), channel_id=1, source_target_pairs={{0,224},{32,0},{64,32},{96,64},{128,96},{160,128},{192,160},{224,1... | collective-permute-start | bytes 2654216 | tf_op jit(solution)/shard_map/ppermute | solution.py:41
  109.6 5.5 %collective-permute-done.25.refs_1_ = bf16[192,1920]{1,0:T(8,128)(2,1)S(1)} collective-permute-done((bf16[192,1920]{1,0:T(8,128)(2,1)S(1)}, bf16[192,1920]{1,0:T(8,128)(2,1)S(1)}, u32[]{:S(2)}, u32[]{:S(2)}) %collective-permute-start.25) | collective-permute-done | bytes 737312 | tf_op jit(solution)/shard_map/ppermute | solution.py:41
  115.1 3.7 %collective-permute-done.26.refs_2_ = bf16[192,1920]{1,0:T(8,128)(2,1)S(1)} collective-permute-done((bf16[192,1920]{1,0:T(8,128)(2,1)S(1)}, bf16[192,1920]{1,0:T(8,128)(2,1)S(1)}, u32[]{:S(2)}, u32[]{:S(2)}) %collective-permute-start.26) | collective-permute-done | bytes 737312 | tf_op jit(solution)/shard_map/ppermute | solution.py:41
  119.2 15.4 %collective-permute-done.23.refs_2_ = bf16[192,1920]{1,0:T(8,128)(2,1)S(1)} collective-permute-done((bf16[192,1920]{1,0:T(8,128)(2,1)S(1)}, bf16[192,1920]{1,0:T(8,128)(2,1)S(1)}, u32[]{:S(2)}, u32[]{:S(2)}) %collective-permute-start.23) | collective-permute-done | bytes 737312 | tf_op jit(solution)/shard_map/ppermute | solution.py:41
  135.0 4.8 %collective-permute-start.9 = (bf16[384,1152]{1,0:T(8,128)(2,1)S(1)}, bf16[384,1152]{1,0:T(8,128)(2,1)S(1)}, u32[]{:S(2)}, u32[]{:S(2)}) collective-permute-start(bf16[384,1152]{1,0:T(8,128)(2,1)S(1)} %collective-permute-done.8.refs_1_), channel_id=1, source_target_pairs={{0,224},{32,0},{64,32},{96,64},{128,96},{160,128},{192,160},{224,1... | collective-permute-start | bytes 2654216 | tf_op jit(solution)/shard_map/ppermute | solution.py:41
  139.8 19.3 %collective-permute-done.27.refs_3_ = bf16[192,1920]{1,0:T(8,128)(2,1)S(1)} collective-permute-done((bf16[192,1920]{1,0:T(8,128)(2,1)S(1)}, bf16[192,1920]{1,0:T(8,128)(2,1)S(1)}, u32[]{:S(2)}, u32[]{:S(2)}) %collective-permute-start.27) | collective-permute-done | bytes 737312 | tf_op jit(solution)/shard_map/ppermute | solution.py:41
  159.1 3.2 %collective-permute-start.24 = (bf16[192,1920]{1,0:T(8,128)(2,1)S(1)}, bf16[192,1920]{1,0:T(8,128)(2,1)S(1)}, u32[]{:S(2)}, u32[]{:S(2)}) collective-permute-start(bf16[192,1920]{1,0:T(8,128)(2,1)S(1)} %collective-permute-done.23.refs_2_), channel_id=1, source_target_pairs={{0,24},{8,0},{16,8},{24,16},{1,25},{9,1},{17,9},{25,17},{2,26},{10... | collective-permute-start | bytes 2211848 | tf_op jit(solution)/shard_map/ppermute | solution.py:41
  164.8 2.1 %collective-permute-start.20 = (bf16[112,1920]{1,0:T(8,128)(2,1)S(1)}, bf16[112,1920]{1,0:T(8,128)(2,1)S(1)}, u32[]{:S(2)}, u32[]{:S(2)}) collective-permute-start(bf16[112,1920]{1,0:T(8,128)(2,1)S(1)} %slice.18), channel_id=1, source_target_pairs={{0,8},{8,16},{16,24},{24,0},{1,9},{9,17},{17,25},{25,1},{2,10},{10... | collective-permute-start | bytes 1290248 | tf_op jit(solution)/shard_map/ppermute | solution.py:41
  168.3 2.8 %shard_map.145 = (bf16[1024,3072]{1,0:T(8,128)(2,1)}, bf16[1024,3072]{1,0:T(8,128)(2,1)}, bf16[3072,1024]{1,0:T(8,128)(2,1)}) custom-call(bf16[384,1152]{1,0:T(8,128)(2,1)} %collective-permute-done.3.refs_0_, bf16[384,1152]{1,0:T(8,128)(2,1)} %collective-permute-done.7.refs_1_, ...), custom_call_target="tpu_custom_call", output_to_operand_aliasing={{0}: (2, {}), {1}: (3, {}), {2}: (4, {})} | custom-call | flops 707788800 | bytes 3538944 | tf_op jit(solution)/shard_map/pallas_call | solution.py:205
  171.1 4.9 %collective-permute-start.10 = (bf16[224,1152]{1,0:T(8,128)(2,1)S(1)}, bf16[224,1152]{1,0:T(8,128)(2,1)S(1)}, u32[]{:S(2)}, u32[]{:S(2)}) collective-permute-start(bf16[224,1152]{1,0:T(8,128)(2,1)S(1)} %slice.17), channel_id=1, source_target_pairs={{0,224},{32,0},{64,32},{96,64},{128,96},{160,128},{192,160},{224,1... | collective-permute-start | bytes 1548296 | tf_op jit(solution)/shard_map/ppermute | solution.py:41
  176.1 3.0 %shard_map.146 = (bf16[1024,3072]{1,0:T(8,128)(2,1)}, bf16[1024,3072]{1,0:T(8,128)(2,1)}, bf16[3072,1024]{1,0:T(8,128)(2,1)}) custom-call(bf16[192,1920]{1,0:T(8,128)(2,1)S(1)} %shard_map.142.refs_0_, bf16[192,1920]{1,0:T(8,128)(2,1)S(1)} %collective-permute-done.25.refs_1_, ...), custom_call_target="tpu_custom_call", output_to_operand_aliasing={{0}: (4, {}), {1}: (5, {}), {2}: (6, {})} | custom-call | flops 1179648000 | bytes 5898240 | tf_op jit(solution)/shard_map/pallas_call | solution.py:205
  179.2 3.0 %shard_map.147 = (bf16[1024,3072]{1,0:T(8,128)(2,1)}, bf16[1024,3072]{1,0:T(8,128)(2,1)}, bf16[3072,1024]{1,0:T(8,128)(2,1)}) custom-call(bf16[192,1920]{1,0:T(8,128)(2,1)S(1)} %shard_map.141.refs_0_, bf16[192,1920]{1,0:T(8,128)(2,1)S(1)} %collective-permute-done.22.refs_1_, ...), custom_call_target="tpu_custom_call", output_to_operand_aliasing={{0}: (4, {}), {1}: (5, {}), {2}: (6, {})} | custom-call | flops 1179648000 | bytes 5898240 | tf_op jit(solution)/shard_map/pallas_call | solution.py:205
  182.2 2.0 %shard_map.148 = (bf16[1024,3072]{1,0:T(8,128)(2,1)}, bf16[1024,3072]{1,0:T(8,128)(2,1)}, bf16[3072,1024]{1,0:T(8,128)(2,1)}) custom-call(bf16[384,1152]{1,0:T(8,128)(2,1)S(1)} %collective-permute-done.4.refs_0_, bf16[384,1152]{1,0:T(8,128)(2,1)S(1)} %collective-permute-done.8.refs_1_, ...), custom_call_target="tpu_custom_call", output_to_operand_aliasing={{0}: (2, {}), {1}: (3, {}), {2}: (4, {})} | custom-call | flops 707788800 | bytes 3538944 | tf_op jit(solution)/shard_map/pallas_call | solution.py:205
  184.2 2.0 %shard_map.149 = (bf16[1024,3072]{1,0:T(8,128)(2,1)}, bf16[1024,3072]{1,0:T(8,128)(2,1)}, bf16[3072,1024]{1,0:T(8,128)(2,1)}) custom-call(bf16[384,1152]{1,0:T(8,128)(2,1)S(1)} %collective-permute-done.5.refs_0_, bf16[384,1152]{1,0:T(8,128)(2,1)S(1)} %collective-permute-done.9.refs_1_, ...), custom_call_target="tpu_custom_call", output_to_operand_aliasing={{0}: (2, {}), {1}: (3, {}), {2}: (4, {})} | custom-call | flops 707788800 | bytes 3538944 | tf_op jit(solution)/shard_map/pallas_call | solution.py:205
  186.3 4.2 %shard_map.150 = (bf16[1024,3072]{1,0:T(8,128)(2,1)}, bf16[1024,3072]{1,0:T(8,128)(2,1)}, bf16[3072,1024]{1,0:T(8,128)(2,1)}) custom-call(bf16[288,1920]{1,0:T(8,128)(2,1)S(1)} %shard_map.140.refs_0_, bf16[288,1920]{1,0:T(8,128)(2,1)S(1)} %collective-permute-done.18.refs_1_, ...), custom_call_target="tpu_custom_call", output_to_operand_aliasing={{0}: (5, {}), {1}: (6, {}), {2}: (7, {})} | custom-call | flops 1769472000 | bytes 8847360 | tf_op jit(solution)/shard_map/pallas_call | solution.py:205
  (81 shorter events, 31.1 us)
Async XLA Ops:
  3.1 16.6 %collective-permute-start = (bf16[96,3072]{1,0:T(8,128)(2,1)}, bf16[96,3072]{1,0:T(8,128)(2,1)S(1)}, u32[]{:S(2)}, u32[]{:S(2)}) collective-permute-start(bf16[96,3072]{1,0:T(8,128)(2,1)} %get-tuple-element.33.refs_0_), channel_id=1, source_target_pairs={{0,8},{8,16},{16,24},{24,0},{1,9},{9,17},{17,25},{25,1},{2,10},{10... | collective-permute-start | bytes 1769480 | tf_op jit(solution)/shard_map/ppermute | solution.py:41
  4.8 15.3 %collective-permute-start.11 = (bf16[96,1920]{1,0:T(8,128)(2,1)}, bf16[96,1920]{1,0:T(8,128)(2,1)S(1)}, u32[]{:S(2)}, u32[]{:S(2)}) collective-permute-start(bf16[96,1920]{1,0:T(8,128)(2,1)} %get-tuple-element.34), channel_id=1, source_target_pairs={{0,32},{32,64},{64,96},{96,128},{128,160},{160,192},{192,224},{224... | collective-permute-start | bytes 1105928 | tf_op jit(solution)/shard_map/ppermute | solution.py:41
  6.7 16.0 %collective-permute-start.14 = (bf16[96,1920]{1,0:T(8,128)(2,1)}, bf16[96,1920]{1,0:T(8,128)(2,1)S(1)}, u32[]{:S(2)}, u32[]{:S(2)}) collective-permute-start(bf16[96,1920]{1,0:T(8,128)(2,1)} %get-tuple-element.34), channel_id=1, source_target_pairs={{0,224},{32,0},{64,32},{96,64},{128,96},{160,128},{192,160},{224,1... | collective-permute-start | bytes 1105928 | tf_op jit(solution)/shard_map/ppermute | solution.py:41
  10.7 22.9 %collective-permute-start.1 = (bf16[96,3072]{1,0:T(8,128)(2,1)}, bf16[96,3072]{1,0:T(8,128)(2,1)S(1)}, u32[]{:S(2)}, u32[]{:S(2)}) collective-permute-start(bf16[96,3072]{1,0:T(8,128)(2,1)} %get-tuple-element.33.refs_0_), channel_id=1, source_target_pairs={{0,24},{8,0},{16,8},{24,16},{1,25},{9,1},{17,9},{25,17},{2,26},{10... | collective-permute-start | bytes 1769480 | tf_op jit(solution)/shard_map/ppermute | solution.py:41
  19.8 15.5 %collective-permute-start.2 = (bf16[96,3072]{1,0:T(8,128)(2,1)S(1)}, bf16[96,3072]{1,0:T(8,128)(2,1)S(1)}, u32[]{:S(2)}, u32[]{:S(2)}) collective-permute-start(bf16[96,3072]{1,0:T(8,128)(2,1)S(1)} %collective-permute-done.refs_1_), channel_id=1, source_target_pairs={{0,8},{8,16},{16,24},{24,0},{1,9},{9,17},{17,25},{25,1},{2,10},{10... | collective-permute-start | bytes 1769480 | tf_op jit(solution)/shard_map/ppermute | solution.py:41
  20.1 13.5 %collective-permute-start.12 = (bf16[96,1920]{1,0:T(8,128)(2,1)S(1)}, bf16[96,1920]{1,0:T(8,128)(2,1)}, u32[]{:S(2)}, u32[]{:S(2)}) collective-permute-start(bf16[96,1920]{1,0:T(8,128)(2,1)S(1)} %collective-permute-done.11.refs_0_), channel_id=1, source_target_pairs={{0,32},{32,64},{64,96},{96,128},{128,160},{160,192},{192,224},{224... | collective-permute-start | bytes 1105928 | tf_op jit(solution)/shard_map/ppermute | solution.py:41
  22.7 19.7 %collective-permute-start.15 = (bf16[96,1920]{1,0:T(8,128)(2,1)S(1)}, bf16[96,1920]{1,0:T(8,128)(2,1)}, u32[]{:S(2)}, u32[]{:S(2)}) collective-permute-start(bf16[96,1920]{1,0:T(8,128)(2,1)S(1)} %collective-permute-done.14.refs_1_), channel_id=1, source_target_pairs={{0,224},{32,0},{64,32},{96,64},{128,96},{160,128},{192,160},{224,1... | collective-permute-start | bytes 1105928 | tf_op jit(solution)/shard_map/ppermute | solution.py:41
  33.5 61.3 %collective-permute-start.13 = (bf16[96,1920]{1,0:T(8,128)(2,1)}, bf16[96,1920]{1,0:T(8,128)(2,1)}, u32[]{:S(2)}, u32[]{:S(2)}) collective-permute-start(bf16[96,1920]{1,0:T(8,128)(2,1)} %collective-permute-done.12.refs_0_), channel_id=1, source_target_pairs={{0,32},{32,64},{64,96},{96,128},{128,160},{160,192},{192,224},{224... | collective-permute-start | bytes 1105928 | tf_op jit(solution)/shard_map/ppermute | solution.py:41
  36.5 69.0 %collective-permute-start.7 = (bf16[384,1152]{1,0:T(8,128)(2,1)S(1)}, bf16[384,1152]{1,0:T(8,128)(2,1)}, u32[]{:S(2)}, u32[]{:S(2)}) collective-permute-start(bf16[384,1152]{1,0:T(8,128)(2,1)S(1)} %shard_map.139.refs_0_), channel_id=1, source_target_pairs={{0,224},{32,0},{64,32},{96,64},{128,96},{160,128},{192,160},{224,1... | collective-permute-start | bytes 2654216 | tf_op jit(solution)/shard_map/ppermute | solution.py:41
  42.5 56.2 %collective-permute-start.16 = (bf16[96,1920]{1,0:T(8,128)(2,1)}, bf16[96,1920]{1,0:T(8,128)(2,1)}, u32[]{:S(2)}, u32[]{:S(2)}) collective-permute-start(bf16[96,1920]{1,0:T(8,128)(2,1)} %collective-permute-done.15.refs_1_), channel_id=1, source_target_pairs={{0,224},{32,0},{64,32},{96,64},{128,96},{160,128},{192,160},{224,1... | collective-permute-start | bytes 1105928 | tf_op jit(solution)/shard_map/ppermute | solution.py:41
  43.5 65.0 %collective-permute-start.3 = (bf16[384,1152]{1,0:T(8,128)(2,1)S(1)}, bf16[384,1152]{1,0:T(8,128)(2,1)}, u32[]{:S(2)}, u32[]{:S(2)}) collective-permute-start(bf16[384,1152]{1,0:T(8,128)(2,1)S(1)} %shard_map.139.refs_0_), channel_id=1, source_target_pairs={{0,32},{32,64},{64,96},{96,128},{128,160},{160,192},{192,224},{224... | collective-permute-start | bytes 2654216 | tf_op jit(solution)/shard_map/ppermute | solution.py:41
  45.4 22.4 %collective-permute-start.28 = (bf16[3072]{0:T(1024)(128)(2,1)S(1)}, bf16[3072]{0:T(1024)(128)(2,1)S(1)}, u32[]{:S(2)}, u32[]{:S(2)}) collective-permute-start(bf16[3072]{0:T(1024)(128)(2,1)S(1)} %dynamic_update_slice.3), channel_id=1, source_target_pairs={{0,224},{32,0},{64,32},{96,64},{128,96},{160,128},{192,160},{224,1... | collective-permute-start | bytes 18440 | tf_op jit(solution)/shard_map/ppermute | solution.py:41
  71.4 5.1 %collective-permute-start.30 = (bf16[3072]{0:T(1024)(128)(2,1)S(1)}, bf16[3072]{0:T(1024)(128)(2,1)S(1)}, u32[]{:S(2)}, u32[]{:S(2)}) collective-permute-start(bf16[3072]{0:T(1024)(128)(2,1)S(1)} %add.45), channel_id=1, source_target_pairs={{0,16},{8,24},{16,0},{24,8},{1,17},{9,25},{17,1},{25,9},{2,18},{10... | collective-permute-start | bytes 18440 | tf_op jit(solution)/shard_map/ppermute | solution.py:41
  85.9 5.1 %collective-permute-start.34 = (bf16[3072]{0:T(1024)(128)(2,1)S(1)}, bf16[3072]{0:T(1024)(128)(2,1)S(1)}, u32[]{:S(2)}, u32[]{:S(2)}) collective-permute-start(bf16[3072]{0:T(1024)(128)(2,1)S(1)} %add.49), channel_id=1, source_target_pairs={{0,4},{2,6},{4,0},{6,2},{1,5},{3,7},{5,1},{7,3},{8,12},{10,14},{12... | collective-permute-start | bytes 18440 | tf_op jit(solution)/shard_map/ppermute | solution.py:41
  91.1 7.6 %collective-permute-start.35 = (bf16[3072]{0:T(1024)(128)(2,1)S(1)}, bf16[3072]{0:T(1024)(128)(2,1)S(1)}, u32[]{:S(2)}, u32[]{:S(2)}) collective-permute-start(bf16[3072]{0:T(1024)(128)(2,1)S(1)} %add.50), channel_id=1, source_target_pairs={{0,128},{32,160},{64,192},{96,224},{128,0},{160,32},{192,64},{224,... | collective-permute-start | bytes 18440 | tf_op jit(solution)/shard_map/ppermute | solution.py:41
  94.9 8.9 %collective-permute-start.17 = (bf16[96,1920]{1,0:T(8,128)(2,1)}, bf16[96,1920]{1,0:T(8,128)(2,1)S(1)}, u32[]{:S(2)}, u32[]{:S(2)}) collective-permute-start(bf16[96,1920]{1,0:T(8,128)(2,1)} %collective-permute-done.13.refs_0_), channel_id=1, source_target_pairs={{0,32},{32,64},{64,96},{96,128},{128,160},{160,192},{192,224},{224... | collective-permute-start | bytes 1105928 | tf_op jit(solution)/shard_map/ppermute | solution.py:41
  98.7 16.4 %collective-permute-start.25 = (bf16[192,1920]{1,0:T(8,128)(2,1)S(1)}, bf16[192,1920]{1,0:T(8,128)(2,1)S(1)}, u32[]{:S(2)}, u32[]{:S(2)}) collective-permute-start(bf16[192,1920]{1,0:T(8,128)(2,1)S(1)} %shard_map.142.refs_0_), channel_id=1, source_target_pairs={{0,8},{8,16},{16,24},{24,0},{1,9},{9,17},{17,25},{25,1},{2,10},{10... | collective-permute-start | bytes 2211848 | tf_op jit(solution)/shard_map/ppermute | solution.py:41
  98.7 20.1 %collective-permute-start.26 = (bf16[192,1920]{1,0:T(8,128)(2,1)S(1)}, bf16[192,1920]{1,0:T(8,128)(2,1)S(1)}, u32[]{:S(2)}, u32[]{:S(2)}) collective-permute-start(bf16[192,1920]{1,0:T(8,128)(2,1)S(1)} %shard_map.142.refs_0_), channel_id=1, source_target_pairs={{0,24},{8,0},{16,8},{24,16},{1,25},{9,1},{17,9},{25,17},{2,26},{10... | collective-permute-start | bytes 2211848 | tf_op jit(solution)/shard_map/ppermute | solution.py:41
  103.8 30.8 %collective-permute-start.23 = (bf16[192,1920]{1,0:T(8,128)(2,1)S(1)}, bf16[192,1920]{1,0:T(8,128)(2,1)S(1)}, u32[]{:S(2)}, u32[]{:S(2)}) collective-permute-start(bf16[192,1920]{1,0:T(8,128)(2,1)S(1)} %shard_map.141.refs_0_), channel_id=1, source_target_pairs={{0,24},{8,0},{16,8},{24,16},{1,25},{9,1},{17,9},{25,17},{2,26},{10... | collective-permute-start | bytes 2211848 | tf_op jit(solution)/shard_map/ppermute | solution.py:41
  105.5 29.4 %collective-permute-start.8 = (bf16[384,1152]{1,0:T(8,128)(2,1)}, bf16[384,1152]{1,0:T(8,128)(2,1)S(1)}, u32[]{:S(2)}, u32[]{:S(2)}) collective-permute-start(bf16[384,1152]{1,0:T(8,128)(2,1)} %collective-permute-done.7.refs_1_), channel_id=1, source_target_pairs={{0,224},{32,0},{64,32},{96,64},{128,96},{160,128},{192,160},{224,1... | collective-permute-start | bytes 2654216 | tf_op jit(solution)/shard_map/ppermute | solution.py:41
  108.5 31.3 %collective-permute-start.4 = (bf16[384,1152]{1,0:T(8,128)(2,1)}, bf16[384,1152]{1,0:T(8,128)(2,1)S(1)}, u32[]{:S(2)}, u32[]{:S(2)}) collective-permute-start(bf16[384,1152]{1,0:T(8,128)(2,1)} %collective-permute-done.3.refs_0_), channel_id=1, source_target_pairs={{0,32},{32,64},{64,96},{96,128},{128,160},{160,192},{192,224},{224... | collective-permute-start | bytes 2654216 | tf_op jit(solution)/shard_map/ppermute | solution.py:41
  115.1 44.0 %collective-permute-start.19 = (bf16[288,1920]{1,0:T(8,128)(2,1)S(1)}, bf16[288,1920]{1,0:T(8,128)(2,1)S(1)}, u32[]{:S(2)}, u32[]{:S(2)}) collective-permute-start(bf16[288,1920]{1,0:T(8,128)(2,1)S(1)} %shard_map.140.refs_0_), channel_id=1, source_target_pairs={{0,24},{8,0},{16,8},{24,16},{1,25},{9,1},{17,9},{25,17},{2,26},{10... | collective-permute-start | bytes 3317768 | tf_op jit(solution)/shard_map/ppermute | solution.py:41
  118.8 43.6 %collective-permute-start.18 = (bf16[288,1920]{1,0:T(8,128)(2,1)S(1)}, bf16[288,1920]{1,0:T(8,128)(2,1)S(1)}, u32[]{:S(2)}, u32[]{:S(2)}) collective-permute-start(bf16[288,1920]{1,0:T(8,128)(2,1)S(1)} %shard_map.140.refs_0_), channel_id=1, source_target_pairs={{0,8},{8,16},{16,24},{24,0},{1,9},{9,17},{17,25},{25,1},{2,10},{10... | collective-permute-start | bytes 3317768 | tf_op jit(solution)/shard_map/ppermute | solution.py:41
  134.6 24.5 %collective-permute-start.27 = (bf16[192,1920]{1,0:T(8,128)(2,1)S(1)}, bf16[192,1920]{1,0:T(8,128)(2,1)S(1)}, u32[]{:S(2)}, u32[]{:S(2)}) collective-permute-start(bf16[192,1920]{1,0:T(8,128)(2,1)S(1)} %collective-permute-done.25.refs_1_), channel_id=1, source_target_pairs={{0,8},{8,16},{16,24},{24,0},{1,9},{9,17},{17,25},{25,1},{2,10},{10... | collective-permute-start | bytes 2211848 | tf_op jit(solution)/shard_map/ppermute | solution.py:41
  135.0 29.8 %collective-permute-start.9 = (bf16[384,1152]{1,0:T(8,128)(2,1)S(1)}, bf16[384,1152]{1,0:T(8,128)(2,1)S(1)}, u32[]{:S(2)}, u32[]{:S(2)}) collective-permute-start(bf16[384,1152]{1,0:T(8,128)(2,1)S(1)} %collective-permute-done.8.refs_1_), channel_id=1, source_target_pairs={{0,224},{32,0},{64,32},{96,64},{128,96},{160,128},{192,160},{224,1... | collective-permute-start | bytes 2654216 | tf_op jit(solution)/shard_map/ppermute | solution.py:41
  139.8 31.4 %collective-permute-start.5 = (bf16[384,1152]{1,0:T(8,128)(2,1)S(1)}, bf16[384,1152]{1,0:T(8,128)(2,1)S(1)}, u32[]{:S(2)}, u32[]{:S(2)}) collective-permute-start(bf16[384,1152]{1,0:T(8,128)(2,1)S(1)} %collective-permute-done.4.refs_0_), channel_id=1, source_target_pairs={{0,32},{32,64},{64,96},{96,128},{128,160},{160,192},{192,224},{224... | collective-permute-start | bytes 2654216 | tf_op jit(solution)/shard_map/ppermute | solution.py:41
  159.1 20.0 %collective-permute-start.22 = (bf16[192,1920]{1,0:T(8,128)(2,1)S(1)}, bf16[192,1920]{1,0:T(8,128)(2,1)S(1)}, u32[]{:S(2)}, u32[]{:S(2)}) collective-permute-start(bf16[192,1920]{1,0:T(8,128)(2,1)S(1)} %shard_map.141.refs_0_), channel_id=1, source_target_pairs={{0,8},{8,16},{16,24},{24,0},{1,9},{9,17},{17,25},{25,1},{2,10},{10... | collective-permute-start | bytes 2211848 | tf_op jit(solution)/shard_map/ppermute | solution.py:41
  159.1 20.1 %collective-permute-start.24 = (bf16[192,1920]{1,0:T(8,128)(2,1)S(1)}, bf16[192,1920]{1,0:T(8,128)(2,1)S(1)}, u32[]{:S(2)}, u32[]{:S(2)}) collective-permute-start(bf16[192,1920]{1,0:T(8,128)(2,1)S(1)} %collective-permute-done.23.refs_2_), channel_id=1, source_target_pairs={{0,24},{8,0},{16,8},{24,16},{1,25},{9,1},{17,9},{25,17},{2,26},{10... | collective-permute-start | bytes 2211848 | tf_op jit(solution)/shard_map/ppermute | solution.py:41
  162.4 23.9 %collective-permute-start.21 = (bf16[176,1920]{1,0:T(8,128)(2,1)S(1)}, bf16[176,1920]{1,0:T(8,128)(2,1)S(1)}, u32[]{:S(2)}, u32[]{:S(2)}) collective-permute-start(bf16[176,1920]{1,0:T(8,128)(2,1)S(1)} %slice.19), channel_id=1, source_target_pairs={{0,24},{8,0},{16,8},{24,16},{1,25},{9,1},{17,9},{25,17},{2,26},{10... | collective-permute-start | bytes 2027528 | tf_op jit(solution)/shard_map/ppermute | solution.py:41
  164.8 21.5 %collective-permute-start.20 = (bf16[112,1920]{1,0:T(8,128)(2,1)S(1)}, bf16[112,1920]{1,0:T(8,128)(2,1)S(1)}, u32[]{:S(2)}, u32[]{:S(2)}) collective-permute-start(bf16[112,1920]{1,0:T(8,128)(2,1)S(1)} %slice.18), channel_id=1, source_target_pairs={{0,8},{8,16},{16,24},{24,0},{1,9},{9,17},{17,25},{25,1},{2,10},{10... | collective-permute-start | bytes 1290248 | tf_op jit(solution)/shard_map/ppermute | solution.py:41
  171.1 19.3 %collective-permute-start.10 = (bf16[224,1152]{1,0:T(8,128)(2,1)S(1)}, bf16[224,1152]{1,0:T(8,128)(2,1)S(1)}, u32[]{:S(2)}, u32[]{:S(2)}) collective-permute-start(bf16[224,1152]{1,0:T(8,128)(2,1)S(1)} %slice.17), channel_id=1, source_target_pairs={{0,224},{32,0},{64,32},{96,64},{128,96},{160,128},{192,160},{224,1... | collective-permute-start | bytes 1548296 | tf_op jit(solution)/shard_map/ppermute | solution.py:41
  179.1 11.4 %collective-permute-start.6 = (bf16[160,1152]{1,0:T(8,128)(2,1)S(1)}, bf16[160,1152]{1,0:T(8,128)(2,1)S(1)}, u32[]{:S(2)}, u32[]{:S(2)}) collective-permute-start(bf16[160,1152]{1,0:T(8,128)(2,1)S(1)} %slice.16), channel_id=1, source_target_pairs={{0,32},{32,64},{64,96},{96,128},{128,160},{160,192},{192,224},{224... | collective-permute-start | bytes 1105928 | tf_op jit(solution)/shard_map/ppermute | solution.py:41
  (10 other events, 167.0 us)
